TPU v7x, 32 devices: a whole 2x2x4 slice. The times are simulated.
32 devices in a mesh: gx: 2 (over y), gy: 4 (over x, core), gz: 4 (over z).
Axes of the slice: x: 2, y: 2, z: 4, core: 2. Of those that a mesh axis runs over, the one named last changes fastest.
Arguments:
- density: float32 [32, 64, 4096], P('gx', 'gy', 'gz'), may hold values from -19 to 19
Outputs:
- potential: float32 [32, 64, 4096], P('gx', 'gy', 'gz')
- coulomb: float32 [64, 64], replicated
All inputs are finite; a program needn't handle non-finite values.
Results may differ from a plain program's by a relative error of at most 0.000057.
Values sent between devices are 32-bit elements; how exact they have to be, the bound alone decides.
No kernel may reach another device: no remote copies, remote signals or barrier semaphores. Data moves between devices by JAX's collectives and lax.ppermute only.
A program may use at most 64 MiB of HBM per device.

v0:
```python
import jax
import jax.numpy as jnp
from jax import lax
from jax.sharding import PartitionSpec as P

PAIRS = 64
LEVELS = 6
COARSE_SWEEPS = 8
OMEGA = 2.0 / 3.0


def extended_2(x, sides, width):
    for axis, dim in sides:
        size, length = (lax.axis_size(axis), x.shape[dim])
        up = [(i, (i + 1) % size) for i in range(size - 1)]
        down = [(j, i) for i, j in up]
        last = lax.slice_in_dim(x, length - width, length, axis=dim)
        initial = lax.slice_in_dim(x, 0, width, axis=dim)
        before = lax.ppermute(last, axis, up)
        after = lax.ppermute(initial, axis, down)
        x = jnp.concatenate([before, x, after], axis=dim)
    return x


def neighbours(padded):
    total = padded[2:, 1:-1, 1:-1] + padded[:-2, 1:-1, 1:-1]
    total = total + padded[1:-1, 2:, 1:-1] + padded[1:-1, :-2, 1:-1]
    return total + padded[1:-1, 1:-1, 2:] + padded[1:-1, 1:-1, :-2]


def apply_inner(padded, factor):
    return factor * (6.0 * padded[1:-1, 1:-1, 1:-1] - neighbours(padded))


def sweep_inner(padded, source, factor):
    return padded[1:-1, 1:-1, 1:-1] + OMEGA * (source - apply_inner(padded, factor)) / (
        6.0 * factor
    )


def zero_rim(current):
    return jnp.pad(current, ((1, 1), (1, 1), (1, 1), (0, 0)))


def restrict(residual):
    size_x, size_y, size_z, count = residual.shape
    grouped = residual.reshape(size_x // 2, 2, size_y // 2, 2, size_z // 2, 2, count)
    return jnp.mean(grouped, axis=(1, 3, 5))


def prolong(correction):
    return jnp.repeat(jnp.repeat(jnp.repeat(correction, 2, axis=0), 2, axis=1), 2, axis=2)


def global_cycle(source, grid_level):
    factor = 0.25 ** (grid_level - 1)
    current = OMEGA * source / (6.0 * factor)
    if grid_level == LEVELS:
        for repeat_no in range(COARSE_SWEEPS - 1):
            current = sweep_inner(zero_rim(current), source, factor)
        return current
    current = sweep_inner(zero_rim(current), source, factor)
    residual = source - apply_inner(zero_rim(current), factor)
    current = current + prolong(global_cycle(restrict(residual), grid_level + 1))
    for repeat_no in range(2):
        current = sweep_inner(zero_rim(current), source, factor)
    return current


def arrange(stacked, block_shape):
    size_x, size_y, size_z, count = block_shape
    devs_x, devs_y, devs_z = (lax.axis_size("gx"), lax.axis_size("gy"), lax.axis_size("gz"))
    grouped = stacked.reshape(devs_x, devs_y, devs_z, size_x, size_y, size_z, count)
    grouped = grouped.transpose(0, 3, 1, 4, 2, 5, 6)
    return grouped.reshape(devs_x * size_x, devs_y * size_y, devs_z * size_z, count)


def own_block(gathered, block_shape):
    size_x, size_y, size_z, count = block_shape
    starts = (
        lax.axis_index("gx") * size_x,
        lax.axis_index("gy") * size_y,
        lax.axis_index("gz") * size_z,
        jnp.int32(0),
    )
    return lax.dynamic_slice(gathered, starts, block_shape)


def edge_mask(length, where, devices):
    position = jnp.arange(length + 2, dtype=jnp.int32) - 1 + where * length
    return (position >= 0) & (position < length * devices)


def inside_mask(block_shape):
    mask_x = edge_mask(block_shape[0], lax.axis_index("gx"), lax.axis_size("gx"))
    mask_y = edge_mask(block_shape[1], lax.axis_index("gy"), lax.axis_size("gy"))
    mask_z = edge_mask(block_shape[2], lax.axis_index("gz"), lax.axis_size("gz"))
    joined = mask_x[:, None, None] & mask_y[None, :, None] & mask_z[None, None, :]
    return joined[..., None].astype(jnp.float32)


def double_sweep(current, source, factor):
    count = current.shape[3]
    extended = extended_2(
        jnp.concatenate([current, source], axis=3), (("gx", 0), ("gy", 1), ("gz", 2)), 2
    )
    source_wide = extended[1:-1, 1:-1, 1:-1, count:]
    swept = sweep_inner(extended[..., :count], source_wide, factor) * inside_mask(current.shape)
    return swept


def distributed(source, grid_level):
    factor = 0.25 ** (grid_level - 1)
    if grid_level == LEVELS - 1:
        stacked = lax.all_gather(source[None], ("gx", "gy", "gz"), axis=0, tiled=True)
        return own_block(global_cycle(arrange(stacked, source.shape), grid_level), source.shape)
    current = OMEGA * source / (6.0 * factor)
    swept = double_sweep(current, source, factor)
    residual = source - apply_inner(swept, factor)
    current = swept[1:-1, 1:-1, 1:-1]
    current = current + prolong(distributed(restrict(residual), grid_level + 1))
    current = sweep_inner(double_sweep(current, source, factor), source, factor)
    return current


def local(density):
    cells_x, cells_y, merged = density.shape
    cells_z = merged // PAIRS
    cells = density.reshape(cells_x, cells_y, cells_z, PAIRS)
    solved = distributed(cells, 1)
    partial_block = jnp.dot(
        cells.reshape(-1, PAIRS).T,
        solved.reshape(-1, PAIRS),
        precision=lax.Precision.HIGHEST,
        preferred_element_type=jnp.float32,
    )
    summed = lax.psum(partial_block, ("gx", "gy", "gz"))
    total_cells = (
        cells_x
        * cells_y
        * cells_z
        * lax.axis_size("gx")
        * lax.axis_size("gy")
        * lax.axis_size("gz")
    )
    coulomb = summed * (4.0 / total_cells)
    return (solved.reshape(cells_x, cells_y, merged), coulomb)


def solution(mesh):
    return jax.shard_map(
        local,
        mesh=mesh,
        in_specs=(P("gx", "gy", "gz"),),
        out_specs=(P("gx", "gy", "gz"), P()),
        check_vma=False,
    )
```

profile of v0, /device:TPU:14, one launch (start us, length us, event | category | flops | bytes accessed | tf_op | source)
XLA Modules:
  0.0 362.6 jit_solution(3952595412670936373)
XLA Ops:
  6.1 4.6 %collective-permute-start.1 = (f32[2,16,16,128]{3,2,1,0:T(8,128)S(1)}, f32[2,16,16,128]{3,2,1,0:T(8,128)S(1)}, u32[]{:S(2)}, u32[]{:S(2)}) collective-permute-start(f32[2,16,16,128]{3,2,1,0:T(8,128)S(1)} %get-tuple-element.10), channel_id=1, source_target_pairs={{16,0},{17,1},{18,2},{19,3},{20,4},{21,5},{22,6},{23,7},{24,8},{25... | collective-permute-start | bytes 786440 | tf_op jit(solution)/shard_map/ppermute | solution.py:20
  10.7 4.0 %collective-permute-done = f32[2,16,16,128]{3,2,1,0:T(8,128)S(1)} collective-permute-done((f32[2,16,16,128]{3,2,1,0:T(8,128)S(1)}, f32[2,16,16,128]{3,2,1,0:T(8,128)S(1)}, u32[]{:S(2)}, u32[]{:S(2)}) %collective-permute-start) | collective-permute-done | bytes 262176 | tf_op jit(solution)/shard_map/ppermute | solution.py:19
  15.9 2.2 fusion.55
  18.2 1.9 collective-permute-start.2
  20.1 3.6 %collective-permute-start.3 = (f32[20,2,16,128]{3,2,1,0:T(8,128)S(1)}, f32[20,2,16,128]{3,2,1,0:T(8,128)S(1)}, u32[]{:S(2)}, u32[]{:S(2)}) collective-permute-start(f32[20,2,16,128]{3,2,1,0:T(8,128)S(1)} %get-tuple-element.19), channel_id=1, source_target_pairs={{4,0},{8,4},{12,8},{5,1},{9,5},{13,9},{6,2},{10,6},{14,10},{7,3},{... | collective-permute-start | bytes 983048 | tf_op jit(solution)/shard_map/ppermute | solution.py:20
  23.9 2.7 collective-permute-done.2
  29.3 3.5 collective-permute-start.4
  32.8 2.4 collective-permute-start.5
  35.4 3.8 %collective-permute-done.4 = f32[20,20,2,128]{3,2,1,0:T(2,128)S(1)} collective-permute-done((f32[20,20,2,128]{3,2,1,0:T(2,128)S(1)}, f32[20,20,2,128]{3,2,1,0:T(2,128)S(1)}, u32[]{:S(2)}, u32[]{:S(2)}) %collective-permute-start.4) | collective-permute-done | bytes 409632 | tf_op jit(solution)/shard_map/ppermute | solution.py:19
  39.2 3.5 collective-permute-done.5
  42.7 3.2 fusion.5
  45.9 8.6 %fusion.23 = f32[18,18,18,64]{3,2,1,0:T(8,128)S(1)} fusion(f32[16,16,16,64]{3,2,1,0:T(8,128)S(1)} %reshape.351, f32[20,20,2,128]{3,2,1,0:T(2,128)S(1)} %collective-permute-done.4, f32[20,2,16,128]{3,2,1,0:T(8,128)S(1)} %collective-permute-done.3, f32[20,2,16,128]{3,2,1,0:T(8,128)S(1)} %collective-permute-done.2, ...), kind=kLoop, calls=%fused_computation.29 | loop fusion | flops 8584704 | bytes 14570272 | tf_op jit(solution)/shard_map/mul | solution.py:108
  54.5 2.6 fusion.63
  57.1 3.0 reduce_sum.52
  62.2 4.5 %collective-permute-start.7 = (f32[2,8,8,128]{3,2,1,0:T(8,128)S(1)}, f32[2,8,8,128]{3,2,1,0:T(8,128)S(1)}, u32[]{:S(2)}, u32[]{:S(2)}) collective-permute-start(f32[2,8,8,128]{3,2,1,0:T(8,128)S(1)} %get-tuple-element.8), channel_id=1, source_target_pairs={{16,0},{17,1},{18,2},{19,3},{20,4},{21,5},{22,6},{23,7},{24,8},{25... | collective-permute-start | bytes 196616 | tf_op jit(solution)/shard_map/ppermute | solution.py:20
  68.8 1.9 collective-permute-start.8
  70.7 3.6 %collective-permute-start.9 = (f32[12,2,8,128]{3,2,1,0:T(8,128)S(1)}, f32[12,2,8,128]{3,2,1,0:T(8,128)S(1)}, u32[]{:S(2)}, u32[]{:S(2)}) collective-permute-start(f32[12,2,8,128]{3,2,1,0:T(8,128)S(1)} %get-tuple-element.30), channel_id=1, source_target_pairs={{4,0},{8,4},{12,8},{5,1},{9,5},{13,9},{6,2},{10,6},{14,10},{7,3},{... | collective-permute-start | bytes 294920 | tf_op jit(solution)/shard_map/ppermute | solution.py:20
  76.8 3.5 collective-permute-start.10
  80.3 2.4 collective-permute-start.11
  83.9 3.5 collective-permute-done.11
  91.2 4.7 %collective-permute-start.13 = (f32[2,4,4,128]{3,2,1,0:T(4,128)S(1)}, f32[2,4,4,128]{3,2,1,0:T(4,128)S(1)}, u32[]{:S(2)}, u32[]{:S(2)}) collective-permute-start(f32[2,4,4,128]{3,2,1,0:T(4,128)S(1)} %get-tuple-element.47), channel_id=1, source_target_pairs={{16,0},{17,1},{18,2},{19,3},{20,4},{21,5},{22,6},{23,7},{24,8},{25... | collective-permute-start | bytes 49160 | tf_op jit(solution)/shard_map/ppermute | solution.py:20
  97.2 1.9 collective-permute-start.14
  99.2 3.6 %collective-permute-start.15 = (f32[8,2,4,128]{3,2,1,0:T(4,128)S(1)}, f32[8,2,4,128]{3,2,1,0:T(4,128)S(1)}, u32[]{:S(2)}, u32[]{:S(2)}) collective-permute-start(f32[8,2,4,128]{3,2,1,0:T(4,128)S(1)} %get-tuple-element.45), channel_id=1, source_target_pairs={{4,0},{8,4},{12,8},{5,1},{9,5},{13,9},{6,2},{10,6},{14,10},{7,3},{... | collective-permute-start | bytes 98312 | tf_op jit(solution)/shard_map/ppermute | solution.py:20
  104.6 1.9 collective-permute-start.16
  106.5 3.9 %collective-permute-start.17 = (f32[8,8,2,128]{3,2,1,0:T(2,128)S(1)}, f32[8,8,2,128]{3,2,1,0:T(2,128)S(1)}, u32[]{:S(2)}, u32[]{:S(2)}) collective-permute-start(f32[8,8,2,128]{3,2,1,0:T(2,128)S(1)} %get-tuple-element.38), channel_id=1, source_target_pairs={{1,0},{2,1},{3,2},{5,4},{6,5},{7,6},{9,8},{10,9},{11,10},{13,12},{... | collective-permute-start | bytes 196616 | tf_op jit(solution)/shard_map/ppermute | solution.py:20
  114.4 4.5 %collective-permute-start.19 = (f32[2,2,2,128]{3,2,1,0:T(2,128)S(1)}, f32[2,2,2,128]{3,2,1,0:T(2,128)S(1)}, u32[]{:S(2)}, u32[]{:S(2)}) collective-permute-start(f32[2,2,2,128]{3,2,1,0:T(2,128)S(1)} %pad_maximum_fusion.46), channel_id=1, source_target_pairs={{16,0},{17,1},{18,2},{19,3},{20,4},{21,5},{22,6},{23,7},{24,8},{25... | collective-permute-start | bytes 12296 | tf_op jit(solution)/shard_map/ppermute | solution.py:20
  120.3 1.9 collective-permute-start.20
  122.3 3.6 %collective-permute-start.21 = (f32[6,2,2,128]{3,2,1,0:T(2,128)S(1)}, f32[6,2,2,128]{3,2,1,0:T(2,128)S(1)}, u32[]{:S(2)}, u32[]{:S(2)}) collective-permute-start(f32[6,2,2,128]{3,2,1,0:T(2,128)S(1)} %fusion.281), channel_id=1, source_target_pairs={{4,0},{8,4},{12,8},{5,1},{9,5},{13,9},{6,2},{10,6},{14,10},{7,3},{... | collective-permute-start | bytes 36872 | tf_op jit(solution)/shard_map/ppermute | solution.py:20
  129.9 3.9 %collective-permute-start.23 = (f32[6,6,2,128]{3,2,1,0:T(2,128)}, f32[6,6,2,128]{3,2,1,0:T(2,128)}, u32[]{:S(2)}, u32[]{:S(2)}) collective-permute-start(f32[6,6,2,128]{3,2,1,0:T(2,128)} %fusion.211), channel_id=1, source_target_pairs={{1,0},{2,1},{3,2},{5,4},{6,5},{7,6},{9,8},{10,9},{11,10},{13,12},{... | collective-permute-start | bytes 110600 | tf_op jit(solution)/shard_map/ppermute | solution.py:20
  134.0 2.0 collective-permute-done.23
  138.5 42.3 %all-reduce.11 = f32[2048]{0:T(1024)S(1)} all-reduce(f32[2048]{0:T(1024)S(1)} %multiply_dynamic-update-slice_fusion), channel_id=2, replica_groups=mesh['gx'=2,'gy'=4,'gz'=4] {'gx','gy','gz'}, use_global_device_ids=true, to_apply=%add.11 | all-reduce | flops 2048 | bytes 16384
  183.3 4.5 %collective-permute-start.25 = (f32[2,2,2,128]{3,2,1,0:T(2,128)S(1)}, f32[2,2,2,128]{3,2,1,0:T(2,128)S(1)}, u32[]{:S(2)}, u32[]{:S(2)}) collective-permute-start(f32[2,2,2,128]{3,2,1,0:T(2,128)S(1)} %pad_maximum_fusion.47), channel_id=1, source_target_pairs={{16,0},{17,1},{18,2},{19,3},{20,4},{21,5},{22,6},{23,7},{24,8},{25... | collective-permute-start | bytes 12296 | tf_op jit(solution)/shard_map/ppermute | solution.py:20
  189.3 1.9 collective-permute-start.26
  191.2 3.6 %collective-permute-start.27 = (f32[6,2,2,128]{3,2,1,0:T(2,128)S(1)}, f32[6,2,2,128]{3,2,1,0:T(2,128)S(1)}, u32[]{:S(2)}, u32[]{:S(2)}) collective-permute-start(f32[6,2,2,128]{3,2,1,0:T(2,128)S(1)} %fusion.283), channel_id=1, source_target_pairs={{4,0},{8,4},{12,8},{5,1},{9,5},{13,9},{6,2},{10,6},{14,10},{7,3},{... | collective-permute-start | bytes 36872 | tf_op jit(solution)/shard_map/ppermute | solution.py:20
  196.3 2.5 collective-permute-start.28
  198.8 3.3 collective-permute-start.29
  202.1 2.6 collective-permute-done.29
  206.4 4.5 %collective-permute-start.31 = (f32[2,4,4,128]{3,2,1,0:T(4,128)S(1)}, f32[2,4,4,128]{3,2,1,0:T(4,128)S(1)}, u32[]{:S(2)}, u32[]{:S(2)}) collective-permute-start(f32[2,4,4,128]{3,2,1,0:T(4,128)S(1)} %get-tuple-element.43), channel_id=1, source_target_pairs={{16,0},{17,1},{18,2},{19,3},{20,4},{21,5},{22,6},{23,7},{24,8},{25... | collective-permute-start | bytes 49160 | tf_op jit(solution)/shard_map/ppermute | solution.py:20
  212.5 1.9 collective-permute-start.32
  214.4 3.6 %collective-permute-start.33 = (f32[8,2,4,128]{3,2,1,0:T(4,128)S(1)}, f32[8,2,4,128]{3,2,1,0:T(4,128)S(1)}, u32[]{:S(2)}, u32[]{:S(2)}) collective-permute-start(f32[8,2,4,128]{3,2,1,0:T(4,128)S(1)} %get-tuple-element.41), channel_id=1, source_target_pairs={{4,0},{8,4},{12,8},{5,1},{9,5},{13,9},{6,2},{10,6},{14,10},{7,3},{... | collective-permute-start | bytes 98312 | tf_op jit(solution)/shard_map/ppermute | solution.py:20
  219.8 1.9 collective-permute-start.34
  221.7 3.9 %collective-permute-start.35 = (f32[8,8,2,128]{3,2,1,0:T(2,128)S(1)}, f32[8,8,2,128]{3,2,1,0:T(2,128)S(1)}, u32[]{:S(2)}, u32[]{:S(2)}) collective-permute-start(f32[8,8,2,128]{3,2,1,0:T(2,128)S(1)} %get-tuple-element.36), channel_id=1, source_target_pairs={{1,0},{2,1},{3,2},{5,4},{6,5},{7,6},{9,8},{10,9},{11,10},{13,12},{... | collective-permute-start | bytes 196616 | tf_op jit(solution)/shard_map/ppermute | solution.py:20
  225.9 1.9 collective-permute-done.35
  230.5 4.5 %collective-permute-start.37 = (f32[2,8,8,128]{3,2,1,0:T(8,128)S(1)}, f32[2,8,8,128]{3,2,1,0:T(8,128)S(1)}, u32[]{:S(2)}, u32[]{:S(2)}) collective-permute-start(f32[2,8,8,128]{3,2,1,0:T(8,128)S(1)} %get-tuple-element.32), channel_id=1, source_target_pairs={{16,0},{17,1},{18,2},{19,3},{20,4},{21,5},{22,6},{23,7},{24,8},{25... | collective-permute-start | bytes 196616 | tf_op jit(solution)/shard_map/ppermute | solution.py:20
  237.2 1.9 collective-permute-start.38
  239.1 3.6 %collective-permute-start.39 = (f32[12,2,8,128]{3,2,1,0:T(8,128)S(1)}, f32[12,2,8,128]{3,2,1,0:T(8,128)S(1)}, u32[]{:S(2)}, u32[]{:S(2)}) collective-permute-start(f32[12,2,8,128]{3,2,1,0:T(8,128)S(1)} %get-tuple-element.28), channel_id=1, source_target_pairs={{4,0},{8,4},{12,8},{5,1},{9,5},{13,9},{6,2},{10,6},{14,10},{7,3},{... | collective-permute-start | bytes 294920 | tf_op jit(solution)/shard_map/ppermute | solution.py:20
  245.2 1.9 collective-permute-start.40
  247.1 3.9 %collective-permute-start.41 = (f32[12,12,2,128]{3,2,1,0:T(2,128)S(1)}, f32[12,12,2,128]{3,2,1,0:T(2,128)S(1)}, u32[]{:S(2)}, u32[]{:S(2)}) collective-permute-start(f32[12,12,2,128]{3,2,1,0:T(2,128)S(1)} %get-tuple-element.23), channel_id=1, source_target_pairs={{1,0},{2,1},{3,2},{5,4},{6,5},{7,6},{9,8},{10,9},{11,10},{13,12},{... | collective-permute-start | bytes 442376 | tf_op jit(solution)/shard_map/ppermute | solution.py:20
  252.2 1.9 collective-permute-done.41
  260.1 4.6 %collective-permute-start.43 = (f32[2,16,16,128]{3,2,1,0:T(8,128)S(1)}, f32[2,16,16,128]{3,2,1,0:T(8,128)S(1)}, u32[]{:S(2)}, u32[]{:S(2)}) collective-permute-start(f32[2,16,16,128]{3,2,1,0:T(8,128)S(1)} %get-tuple-element.21), channel_id=1, source_target_pairs={{16,0},{17,1},{18,2},{19,3},{20,4},{21,5},{22,6},{23,7},{24,8},{25... | collective-permute-start | bytes 786440 | tf_op jit(solution)/shard_map/ppermute | solution.py:20
  264.7 2.4 collective-permute-done.42
  269.3 1.9 collective-permute-start.44
  271.2 3.6 %collective-permute-start.45 = (f32[20,2,16,128]{3,2,1,0:T(8,128)S(1)}, f32[20,2,16,128]{3,2,1,0:T(8,128)S(1)}, u32[]{:S(2)}, u32[]{:S(2)}) collective-permute-start(f32[20,2,16,128]{3,2,1,0:T(8,128)S(1)} %get-tuple-element.17), channel_id=1, source_target_pairs={{4,0},{8,4},{12,8},{5,1},{9,5},{13,9},{6,2},{10,6},{14,10},{7,3},{... | collective-permute-start | bytes 983048 | tf_op jit(solution)/shard_map/ppermute | solution.py:20
  274.8 2.8 collective-permute-done.44
  281.3 1.9 collective-permute-start.46
  283.2 4.9 %collective-permute-start.47 = (f32[20,20,2,128]{3,2,1,0:T(2,128)}, f32[20,20,2,128]{3,2,1,0:T(2,128)}, u32[]{:S(2)}, u32[]{:S(2)}) collective-permute-start(f32[20,20,2,128]{3,2,1,0:T(2,128)} %get-tuple-element.12), channel_id=1, source_target_pairs={{1,0},{2,1},{3,2},{5,4},{6,5},{7,6},{9,8},{10,9},{11,10},{13,12},{... | collective-permute-start | bytes 1228808 | tf_op jit(solution)/shard_map/ppermute | solution.py:20
  288.1 2.8 reshape_reshape.3
  291.4 2.2 collective-permute-done.47
  293.6 4.6 %fusion.11 = f32[20,20,20,128]{3,2,1,0:T(8,128)S(1)} fusion(f32[16,16,16,64]{3,2,1,0:T(8,128)S(1)} %reshape.351, f32[20,20,2,128]{3,2,1,0:T(2,128)} %collective-permute-done.47, f32[20,2,16,128]{3,2,1,0:T(8,128)S(1)} %collective-permute-done.45, f32[2,16,16,128]{3,2,1,0:T(8,128)S(1)} %collective-permute-done.43, f32[16,16,16,64]{3,2,1,0:T(8,128)} %copy-done.4, ...), kind=kLoop, calls=%fused_computation.13 | loop fusion | flops 7168000 | bytes 8192000 | tf_op jit(solution)/shard_map/concatenate | solution.py:21
  298.2 9.5 %fusion.35 = f32[18,18,18,64]{3,2,1,0:T(8,128)S(1)} fusion(f32[16,16,16,64]{3,2,1,0:T(8,128)S(1)} %reshape.351, f32[20,20,2,128]{3,2,1,0:T(2,128)} %collective-permute-done.46, f32[20,2,16,128]{3,2,1,0:T(8,128)S(1)} %collective-permute-done.45, f32[20,2,16,128]{3,2,1,0:T(8,128)S(1)} %collective-permute-done.44, ...), kind=kLoop, calls=%fused_computation.41 | loop fusion | flops 8584704 | bytes 14570272 | tf_op jit(solution)/shard_map/mul | solution.py:108
  307.7 3.1 fusion.61
  310.8 2.9 reshape.365
  313.7 5.2 %convolution_bitcast_fusion = f32[64,64]{0,1:T(8,128)S(1)} fusion(f32[4096,64]{1,0:T(8,128)S(1)} %bitcast.73, f32[4096,64]{1,0:T(8,128)} %reshape_reshape.3), kind=kOutput, calls=%fused_computation.108 | convolution fusion | flops 201326592 | bytes 2113536 | tf_op jit(solution)/shard_map/dot_general | solution.py:131
  318.9 43.0 %psum.7 = f32[64,64]{0,1:T(8,128)S(1)} all-reduce(f32[64,64]{0,1:T(8,128)S(1)} %convolution_bitcast_fusion), channel_id=1, replica_groups=mesh['gx'=2,'gy'=4,'gz'=4] {'gx','gy','gz'}, use_global_device_ids=true, to_apply=%region_6.7 | all-reduce | flops 4096 | bytes 32768 | tf_op jit(solution)/shard_map/psum | solution.py:137
  (195 shorter events, 67.6 us)
Async XLA Ops:
  4.8 9.9 %collective-permute-start = (f32[2,16,16,128]{3,2,1,0:T(8,128)S(1)}, f32[2,16,16,128]{3,2,1,0:T(8,128)S(1)}, u32[]{:S(2)}, u32[]{:S(2)}) collective-permute-start(f32[2,16,16,128]{3,2,1,0:T(8,128)S(1)} %get-tuple-element.22), channel_id=1, source_target_pairs={{0,16},{1,17},{2,18},{3,19},{4,20},{5,21},{6,22},{7,23},{8,24},{9,... | collective-permute-start | bytes 786440 | tf_op jit(solution)/shard_map/ppermute | solution.py:19
  6.1 9.8 %collective-permute-start.1 = (f32[2,16,16,128]{3,2,1,0:T(8,128)S(1)}, f32[2,16,16,128]{3,2,1,0:T(8,128)S(1)}, u32[]{:S(2)}, u32[]{:S(2)}) collective-permute-start(f32[2,16,16,128]{3,2,1,0:T(8,128)S(1)} %get-tuple-element.10), channel_id=1, source_target_pairs={{16,0},{17,1},{18,2},{19,3},{20,4},{21,5},{22,6},{23,7},{24,8},{25... | collective-permute-start | bytes 786440 | tf_op jit(solution)/shard_map/ppermute | solution.py:20
  10.7 17.6 %copy-start.3 = (f32[16,16,16,64]{3,2,1,0:T(8,128)S(1)}, f32[16,16,16,64]{3,2,1,0:T(8,128)}, u32[]{:S(2)}) copy-start(f32[16,16,16,64]{3,2,1,0:T(8,128)} %copy-done.2) | copy-start | bytes 3145732
  18.2 8.4 %collective-permute-start.2 = (f32[20,2,16,128]{3,2,1,0:T(8,128)S(1)}, f32[20,2,16,128]{3,2,1,0:T(8,128)S(1)}, u32[]{:S(2)}, u32[]{:S(2)}) collective-permute-start(f32[20,2,16,128]{3,2,1,0:T(8,128)S(1)} %get-tuple-element.18), channel_id=1, source_target_pairs={{0,4},{4,8},{8,12},{1,5},{5,9},{9,13},{2,6},{6,10},{10,14},{3,7},{... | collective-permute-start | bytes 983048 | tf_op jit(solution)/shard_map/ppermute | solution.py:19
  20.1 8.2 %collective-permute-start.3 = (f32[20,2,16,128]{3,2,1,0:T(8,128)S(1)}, f32[20,2,16,128]{3,2,1,0:T(8,128)S(1)}, u32[]{:S(2)}, u32[]{:S(2)}) collective-permute-start(f32[20,2,16,128]{3,2,1,0:T(8,128)S(1)} %get-tuple-element.19), channel_id=1, source_target_pairs={{4,0},{8,4},{12,8},{5,1},{9,5},{13,9},{6,2},{10,6},{14,10},{7,3},{... | collective-permute-start | bytes 983048 | tf_op jit(solution)/shard_map/ppermute | solution.py:20
  29.3 9.8 %collective-permute-start.4 = (f32[20,20,2,128]{3,2,1,0:T(2,128)S(1)}, f32[20,20,2,128]{3,2,1,0:T(2,128)S(1)}, u32[]{:S(2)}, u32[]{:S(2)}) collective-permute-start(f32[20,20,2,128]{3,2,1,0:T(2,128)S(1)} %get-tuple-element.15), channel_id=1, source_target_pairs={{0,1},{1,2},{2,3},{4,5},{5,6},{6,7},{8,9},{9,10},{10,11},{12,13},{... | collective-permute-start | bytes 1228808 | tf_op jit(solution)/shard_map/ppermute | solution.py:19
  32.8 9.8 %collective-permute-start.5 = (f32[20,20,2,128]{3,2,1,0:T(2,128)S(1)}, f32[20,20,2,128]{3,2,1,0:T(2,128)S(1)}, u32[]{:S(2)}, u32[]{:S(2)}) collective-permute-start(f32[20,20,2,128]{3,2,1,0:T(2,128)S(1)} %get-tuple-element.14), channel_id=1, source_target_pairs={{1,0},{2,1},{3,2},{5,4},{6,5},{7,6},{9,8},{10,9},{11,10},{13,12},{... | collective-permute-start | bytes 1228808 | tf_op jit(solution)/shard_map/ppermute | solution.py:20
  35.4 10.5 %copy-start.10 = (f32[18,18,18]{2,1,0:T(8,128)}, f32[18,18,18]{2,1,0:T(8,128)S(1)}, u32[]{:S(2)}) copy-start(f32[18,18,18]{2,1,0:T(8,128)S(1)} %and_convert_fusion) | copy-start | bytes 69988
  54.5 2.6 copy-start
  60.1 27.2 %copy-start.7 = (f32[8,8,8,64]{3,2,1,0:T(8,128)}, f32[8,8,8,64]{3,2,1,0:T(8,128)S(1)}, u32[]{:S(2)}) copy-start(f32[8,8,8,64]{3,2,1,0:T(8,128)S(1)} %reduce_sum.52) | copy-start | bytes 393220
  60.9 6.6 %collective-permute-start.6 = (f32[2,8,8,128]{3,2,1,0:T(8,128)S(1)}, f32[2,8,8,128]{3,2,1,0:T(8,128)S(1)}, u32[]{:S(2)}, u32[]{:S(2)}) collective-permute-start(f32[2,8,8,128]{3,2,1,0:T(8,128)S(1)} %get-tuple-element.33), channel_id=1, source_target_pairs={{0,16},{1,17},{2,18},{3,19},{4,20},{5,21},{6,22},{7,23},{8,24},{9,... | collective-permute-start | bytes 196616 | tf_op jit(solution)/shard_map/ppermute | solution.py:19
  62.2 6.4 %collective-permute-start.7 = (f32[2,8,8,128]{3,2,1,0:T(8,128)S(1)}, f32[2,8,8,128]{3,2,1,0:T(8,128)S(1)}, u32[]{:S(2)}, u32[]{:S(2)}) collective-permute-start(f32[2,8,8,128]{3,2,1,0:T(8,128)S(1)} %get-tuple-element.8), channel_id=1, source_target_pairs={{16,0},{17,1},{18,2},{19,3},{20,4},{21,5},{22,6},{23,7},{24,8},{25... | collective-permute-start | bytes 196616 | tf_op jit(solution)/shard_map/ppermute | solution.py:20
  67.5 20.2 %copy-start.14 = (f32[10,10,10]{2,1,0:T(8,128)S(1)}, f32[10,10,10]{2,1,0:T(8,128)}, u32[]{:S(2)}) copy-start(f32[10,10,10]{2,1,0:T(8,128)} %and_convert_fusion.1) | copy-start | bytes 12004
  68.6 18.7 %copy-start.12 = (f32[2,8,8,128]{3,2,1,0:T(8,128)}, f32[2,8,8,128]{3,2,1,0:T(8,128)S(1)}, u32[]{:S(2)}) copy-start(f32[2,8,8,128]{3,2,1,0:T(8,128)S(1)} %collective-permute-done.7) | copy-start | bytes 196612
  68.8 5.9 %collective-permute-start.8 = (f32[12,2,8,128]{3,2,1,0:T(8,128)S(1)}, f32[12,2,8,128]{3,2,1,0:T(8,128)S(1)}, u32[]{:S(2)}, u32[]{:S(2)}) collective-permute-start(f32[12,2,8,128]{3,2,1,0:T(8,128)S(1)} %get-tuple-element.29), channel_id=1, source_target_pairs={{0,4},{4,8},{8,12},{1,5},{5,9},{9,13},{2,6},{6,10},{10,14},{3,7},{... | collective-permute-start | bytes 294920 | tf_op jit(solution)/shard_map/ppermute | solution.py:19
  70.7 5.8 %collective-permute-start.9 = (f32[12,2,8,128]{3,2,1,0:T(8,128)S(1)}, f32[12,2,8,128]{3,2,1,0:T(8,128)S(1)}, u32[]{:S(2)}, u32[]{:S(2)}) collective-permute-start(f32[12,2,8,128]{3,2,1,0:T(8,128)S(1)} %get-tuple-element.30), channel_id=1, source_target_pairs={{4,0},{8,4},{12,8},{5,1},{9,5},{13,9},{6,2},{10,6},{14,10},{7,3},{... | collective-permute-start | bytes 294920 | tf_op jit(solution)/shard_map/ppermute | solution.py:20
  76.8 7.0 %collective-permute-start.10 = (f32[12,12,2,128]{3,2,1,0:T(2,128)S(1)}, f32[12,12,2,128]{3,2,1,0:T(2,128)S(1)}, u32[]{:S(2)}, u32[]{:S(2)}) collective-permute-start(f32[12,12,2,128]{3,2,1,0:T(2,128)S(1)} %get-tuple-element.26), channel_id=1, source_target_pairs={{0,1},{1,2},{2,3},{4,5},{5,6},{6,7},{8,9},{9,10},{10,11},{12,13},{... | collective-permute-start | bytes 442376 | tf_op jit(solution)/shard_map/ppermute | solution.py:19
  80.3 7.0 %collective-permute-start.11 = (f32[12,12,2,128]{3,2,1,0:T(2,128)S(1)}, f32[12,12,2,128]{3,2,1,0:T(2,128)S(1)}, u32[]{:S(2)}, u32[]{:S(2)}) collective-permute-start(f32[12,12,2,128]{3,2,1,0:T(2,128)S(1)} %get-tuple-element.25), channel_id=1, source_target_pairs={{1,0},{2,1},{3,2},{5,4},{6,5},{7,6},{9,8},{10,9},{11,10},{13,12},{... | collective-permute-start | bytes 442376 | tf_op jit(solution)/shard_map/ppermute | solution.py:20
  87.7 1.7 copy-start.8
  89.9 6.1 %collective-permute-start.12 = (f32[2,4,4,128]{3,2,1,0:T(4,128)S(1)}, f32[2,4,4,128]{3,2,1,0:T(4,128)S(1)}, u32[]{:S(2)}, u32[]{:S(2)}) collective-permute-start(f32[2,4,4,128]{3,2,1,0:T(4,128)S(1)} %get-tuple-element.46), channel_id=1, source_target_pairs={{0,16},{1,17},{2,18},{3,19},{4,20},{5,21},{6,22},{7,23},{8,24},{9,... | collective-permute-start | bytes 49160 | tf_op jit(solution)/shard_map/ppermute | solution.py:19
  91.2 6.0 %collective-permute-start.13 = (f32[2,4,4,128]{3,2,1,0:T(4,128)S(1)}, f32[2,4,4,128]{3,2,1,0:T(4,128)S(1)}, u32[]{:S(2)}, u32[]{:S(2)}) collective-permute-start(f32[2,4,4,128]{3,2,1,0:T(4,128)S(1)} %get-tuple-element.47), channel_id=1, source_target_pairs={{16,0},{17,1},{18,2},{19,3},{20,4},{21,5},{22,6},{23,7},{24,8},{25... | collective-permute-start | bytes 49160 | tf_op jit(solution)/shard_map/ppermute | solution.py:20
  97.2 5.7 %collective-permute-start.14 = (f32[8,2,4,128]{3,2,1,0:T(4,128)S(1)}, f32[8,2,4,128]{3,2,1,0:T(4,128)S(1)}, u32[]{:S(2)}, u32[]{:S(2)}) collective-permute-start(f32[8,2,4,128]{3,2,1,0:T(4,128)S(1)} %get-tuple-element.44), channel_id=1, source_target_pairs={{0,4},{4,8},{8,12},{1,5},{5,9},{9,13},{2,6},{6,10},{10,14},{3,7},{... | collective-permute-start | bytes 98312 | tf_op jit(solution)/shard_map/ppermute | solution.py:19
  99.2 5.2 %collective-permute-start.15 = (f32[8,2,4,128]{3,2,1,0:T(4,128)S(1)}, f32[8,2,4,128]{3,2,1,0:T(4,128)S(1)}, u32[]{:S(2)}, u32[]{:S(2)}) collective-permute-start(f32[8,2,4,128]{3,2,1,0:T(4,128)S(1)} %get-tuple-element.45), channel_id=1, source_target_pairs={{4,0},{8,4},{12,8},{5,1},{9,5},{13,9},{6,2},{10,6},{14,10},{7,3},{... | collective-permute-start | bytes 98312 | tf_op jit(solution)/shard_map/ppermute | solution.py:20
  102.9 31.0 %copy-start.17 = (f32[6,6,6]{2,1,0:T(8,128)}, f32[6,6,6]{2,1,0:T(8,128)S(1)}, u32[]{:S(2)}) copy-start(f32[6,6,6]{2,1,0:T(8,128)S(1)} %and_convert_fusion.2) | copy-start | bytes 2596
  104.6 6.4 %collective-permute-start.16 = (f32[8,8,2,128]{3,2,1,0:T(2,128)S(1)}, f32[8,8,2,128]{3,2,1,0:T(2,128)S(1)}, u32[]{:S(2)}, u32[]{:S(2)}) collective-permute-start(f32[8,8,2,128]{3,2,1,0:T(2,128)S(1)} %get-tuple-element.39), channel_id=1, source_target_pairs={{0,1},{1,2},{2,3},{4,5},{5,6},{6,7},{8,9},{9,10},{10,11},{12,13},{... | collective-permute-start | bytes 196616 | tf_op jit(solution)/shard_map/ppermute | solution.py:19
  106.5 6.2 %collective-permute-start.17 = (f32[8,8,2,128]{3,2,1,0:T(2,128)S(1)}, f32[8,8,2,128]{3,2,1,0:T(2,128)S(1)}, u32[]{:S(2)}, u32[]{:S(2)}) collective-permute-start(f32[8,8,2,128]{3,2,1,0:T(2,128)S(1)} %get-tuple-element.38), channel_id=1, source_target_pairs={{1,0},{2,1},{3,2},{5,4},{6,5},{7,6},{9,8},{10,9},{11,10},{13,12},{... | collective-permute-start | bytes 196616 | tf_op jit(solution)/shard_map/ppermute | solution.py:20
  113.1 6.6 %collective-permute-start.18 = (f32[2,2,2,128]{3,2,1,0:T(2,128)S(1)}, f32[2,2,2,128]{3,2,1,0:T(2,128)S(1)}, u32[]{:S(2)}, u32[]{:S(2)}) collective-permute-start(f32[2,2,2,128]{3,2,1,0:T(2,128)S(1)} %pad_maximum_fusion.46), channel_id=1, source_target_pairs={{0,16},{1,17},{2,18},{3,19},{4,20},{5,21},{6,22},{7,23},{8,24},{9,... | collective-permute-start | bytes 12296 | tf_op jit(solution)/shard_map/ppermute | solution.py:19
  114.4 5.9 %collective-permute-start.19 = (f32[2,2,2,128]{3,2,1,0:T(2,128)S(1)}, f32[2,2,2,128]{3,2,1,0:T(2,128)S(1)}, u32[]{:S(2)}, u32[]{:S(2)}) collective-permute-start(f32[2,2,2,128]{3,2,1,0:T(2,128)S(1)} %pad_maximum_fusion.46), channel_id=1, source_target_pairs={{16,0},{17,1},{18,2},{19,3},{20,4},{21,5},{22,6},{23,7},{24,8},{25... | collective-permute-start | bytes 12296 | tf_op jit(solution)/shard_map/ppermute | solution.py:20
  120.3 5.6 %collective-permute-start.20 = (f32[6,2,2,128]{3,2,1,0:T(2,128)S(1)}, f32[6,2,2,128]{3,2,1,0:T(2,128)S(1)}, u32[]{:S(2)}, u32[]{:S(2)}) collective-permute-start(f32[6,2,2,128]{3,2,1,0:T(2,128)S(1)} %fusion.281), channel_id=1, source_target_pairs={{0,4},{4,8},{8,12},{1,5},{5,9},{9,13},{2,6},{6,10},{10,14},{3,7},{... | collective-permute-start | bytes 36872 | tf_op jit(solution)/shard_map/ppermute | solution.py:19
  122.3 5.0 %collective-permute-start.21 = (f32[6,2,2,128]{3,2,1,0:T(2,128)S(1)}, f32[6,2,2,128]{3,2,1,0:T(2,128)S(1)}, u32[]{:S(2)}, u32[]{:S(2)}) collective-permute-start(f32[6,2,2,128]{3,2,1,0:T(2,128)S(1)} %fusion.281), channel_id=1, source_target_pairs={{4,0},{8,4},{12,8},{5,1},{9,5},{13,9},{6,2},{10,6},{14,10},{7,3},{... | collective-permute-start | bytes 36872 | tf_op jit(solution)/shard_map/ppermute | solution.py:20
  128.0 6.0 %collective-permute-start.22 = (f32[6,6,2,128]{3,2,1,0:T(2,128)}, f32[6,6,2,128]{3,2,1,0:T(2,128)S(1)}, u32[]{:S(2)}, u32[]{:S(2)}) collective-permute-start(f32[6,6,2,128]{3,2,1,0:T(2,128)} %fusion.211), channel_id=1, source_target_pairs={{0,1},{1,2},{2,3},{4,5},{5,6},{6,7},{8,9},{9,10},{10,11},{12,13},{... | collective-permute-start | bytes 110600 | tf_op jit(solution)/shard_map/ppermute | solution.py:19
  129.9 6.2 %collective-permute-start.23 = (f32[6,6,2,128]{3,2,1,0:T(2,128)}, f32[6,6,2,128]{3,2,1,0:T(2,128)}, u32[]{:S(2)}, u32[]{:S(2)}) collective-permute-start(f32[6,6,2,128]{3,2,1,0:T(2,128)} %fusion.211), channel_id=1, source_target_pairs={{1,0},{2,1},{3,2},{5,4},{6,5},{7,6},{9,8},{10,9},{11,10},{13,12},{... | collective-permute-start | bytes 110600 | tf_op jit(solution)/shard_map/ppermute | solution.py:20
  133.9 95.2 %copy-start.16 = (f32[2,8,8,128]{3,2,1,0:T(8,128)S(1)}, f32[2,8,8,128]{3,2,1,0:T(8,128)}, u32[]{:S(2)}) copy-start(f32[2,8,8,128]{3,2,1,0:T(8,128)} %get-tuple-element.9) | copy-start | bytes 196612
  182.0 5.8 %collective-permute-start.24 = (f32[2,2,2,128]{3,2,1,0:T(2,128)S(1)}, f32[2,2,2,128]{3,2,1,0:T(2,128)S(1)}, u32[]{:S(2)}, u32[]{:S(2)}) collective-permute-start(f32[2,2,2,128]{3,2,1,0:T(2,128)S(1)} %pad_maximum_fusion.47), channel_id=1, source_target_pairs={{0,16},{1,17},{2,18},{3,19},{4,20},{5,21},{6,22},{7,23},{8,24},{9,... | collective-permute-start | bytes 12296 | tf_op jit(solution)/shard_map/ppermute | solution.py:19
  183.3 5.9 %collective-permute-start.25 = (f32[2,2,2,128]{3,2,1,0:T(2,128)S(1)}, f32[2,2,2,128]{3,2,1,0:T(2,128)S(1)}, u32[]{:S(2)}, u32[]{:S(2)}) collective-permute-start(f32[2,2,2,128]{3,2,1,0:T(2,128)S(1)} %pad_maximum_fusion.47), channel_id=1, source_target_pairs={{16,0},{17,1},{18,2},{19,3},{20,4},{21,5},{22,6},{23,7},{24,8},{25... | collective-permute-start | bytes 12296 | tf_op jit(solution)/shard_map/ppermute | solution.py:20
  189.3 5.6 %collective-permute-start.26 = (f32[6,2,2,128]{3,2,1,0:T(2,128)S(1)}, f32[6,2,2,128]{3,2,1,0:T(2,128)S(1)}, u32[]{:S(2)}, u32[]{:S(2)}) collective-permute-start(f32[6,2,2,128]{3,2,1,0:T(2,128)S(1)} %fusion.283), channel_id=1, source_target_pairs={{0,4},{4,8},{8,12},{1,5},{5,9},{9,13},{2,6},{6,10},{10,14},{3,7},{... | collective-permute-start | bytes 36872 | tf_op jit(solution)/shard_map/ppermute | solution.py:19
  191.2 5.0 %collective-permute-start.27 = (f32[6,2,2,128]{3,2,1,0:T(2,128)S(1)}, f32[6,2,2,128]{3,2,1,0:T(2,128)S(1)}, u32[]{:S(2)}, u32[]{:S(2)}) collective-permute-start(f32[6,2,2,128]{3,2,1,0:T(2,128)S(1)} %fusion.283), channel_id=1, source_target_pairs={{4,0},{8,4},{12,8},{5,1},{9,5},{13,9},{6,2},{10,6},{14,10},{7,3},{... | collective-permute-start | bytes 36872 | tf_op jit(solution)/shard_map/ppermute | solution.py:20
  196.3 5.8 %collective-permute-start.28 = (f32[6,6,2,128]{3,2,1,0:T(2,128)S(1)}, f32[6,6,2,128]{3,2,1,0:T(2,128)S(1)}, u32[]{:S(2)}, u32[]{:S(2)}) collective-permute-start(f32[6,6,2,128]{3,2,1,0:T(2,128)S(1)} %fusion.215), channel_id=1, source_target_pairs={{0,1},{1,2},{2,3},{4,5},{5,6},{6,7},{8,9},{9,10},{10,11},{12,13},{... | collective-permute-start | bytes 110600 | tf_op jit(solution)/shard_map/ppermute | solution.py:19
  198.8 5.9 %collective-permute-start.29 = (f32[6,6,2,128]{3,2,1,0:T(2,128)S(1)}, f32[6,6,2,128]{3,2,1,0:T(2,128)S(1)}, u32[]{:S(2)}, u32[]{:S(2)}) collective-permute-start(f32[6,6,2,128]{3,2,1,0:T(2,128)S(1)} %fusion.215), channel_id=1, source_target_pairs={{1,0},{2,1},{3,2},{5,4},{6,5},{7,6},{9,8},{10,9},{11,10},{13,12},{... | collective-permute-start | bytes 110600 | tf_op jit(solution)/shard_map/ppermute | solution.py:20
  205.1 5.9 %collective-permute-start.30 = (f32[2,4,4,128]{3,2,1,0:T(4,128)S(1)}, f32[2,4,4,128]{3,2,1,0:T(4,128)S(1)}, u32[]{:S(2)}, u32[]{:S(2)}) collective-permute-start(f32[2,4,4,128]{3,2,1,0:T(4,128)S(1)} %get-tuple-element.42), channel_id=1, source_target_pairs={{0,16},{1,17},{2,18},{3,19},{4,20},{5,21},{6,22},{7,23},{8,24},{9,... | collective-permute-start | bytes 49160 | tf_op jit(solution)/shard_map/ppermute | solution.py:19
  206.4 6.0 %collective-permute-start.31 = (f32[2,4,4,128]{3,2,1,0:T(4,128)S(1)}, f32[2,4,4,128]{3,2,1,0:T(4,128)S(1)}, u32[]{:S(2)}, u32[]{:S(2)}) collective-permute-start(f32[2,4,4,128]{3,2,1,0:T(4,128)S(1)} %get-tuple-element.43), channel_id=1, source_target_pairs={{16,0},{17,1},{18,2},{19,3},{20,4},{21,5},{22,6},{23,7},{24,8},{25... | collective-permute-start | bytes 49160 | tf_op jit(solution)/shard_map/ppermute | solution.py:20
  212.5 5.6 %collective-permute-start.32 = (f32[8,2,4,128]{3,2,1,0:T(4,128)S(1)}, f32[8,2,4,128]{3,2,1,0:T(4,128)S(1)}, u32[]{:S(2)}, u32[]{:S(2)}) collective-permute-start(f32[8,2,4,128]{3,2,1,0:T(4,128)S(1)} %get-tuple-element.40), channel_id=1, source_target_pairs={{0,4},{4,8},{8,12},{1,5},{5,9},{9,13},{2,6},{6,10},{10,14},{3,7},{... | collective-permute-start | bytes 98312 | tf_op jit(solution)/shard_map/ppermute | solution.py:19
  214.4 5.2 %collective-permute-start.33 = (f32[8,2,4,128]{3,2,1,0:T(4,128)S(1)}, f32[8,2,4,128]{3,2,1,0:T(4,128)S(1)}, u32[]{:S(2)}, u32[]{:S(2)}) collective-permute-start(f32[8,2,4,128]{3,2,1,0:T(4,128)S(1)} %get-tuple-element.41), channel_id=1, source_target_pairs={{4,0},{8,4},{12,8},{5,1},{9,5},{13,9},{6,2},{10,6},{14,10},{7,3},{... | collective-permute-start | bytes 98312 | tf_op jit(solution)/shard_map/ppermute | solution.py:20
  219.8 6.2 %collective-permute-start.34 = (f32[8,8,2,128]{3,2,1,0:T(2,128)S(1)}, f32[8,8,2,128]{3,2,1,0:T(2,128)S(1)}, u32[]{:S(2)}, u32[]{:S(2)}) collective-permute-start(f32[8,8,2,128]{3,2,1,0:T(2,128)S(1)} %get-tuple-element.37), channel_id=1, source_target_pairs={{0,1},{1,2},{2,3},{4,5},{5,6},{6,7},{8,9},{9,10},{10,11},{12,13},{... | collective-permute-start | bytes 196616 | tf_op jit(solution)/shard_map/ppermute | solution.py:19
  221.7 6.2 %collective-permute-start.35 = (f32[8,8,2,128]{3,2,1,0:T(2,128)S(1)}, f32[8,8,2,128]{3,2,1,0:T(2,128)S(1)}, u32[]{:S(2)}, u32[]{:S(2)}) collective-permute-start(f32[8,8,2,128]{3,2,1,0:T(2,128)S(1)} %get-tuple-element.36), channel_id=1, source_target_pairs={{1,0},{2,1},{3,2},{5,4},{6,5},{7,6},{9,8},{10,9},{11,10},{13,12},{... | collective-permute-start | bytes 196616 | tf_op jit(solution)/shard_map/ppermute | solution.py:20
  229.1 25.3 %copy-start.15 = (f32[10,10,10]{2,1,0:T(8,128)S(1)}, f32[10,10,10]{2,1,0:T(8,128)}, u32[]{:S(2)}) copy-start(f32[10,10,10]{2,1,0:T(8,128)} %and_convert_fusion.1) | copy-start | bytes 12004
  229.3 6.2 %collective-permute-start.36 = (f32[2,8,8,128]{3,2,1,0:T(8,128)S(1)}, f32[2,8,8,128]{3,2,1,0:T(8,128)S(1)}, u32[]{:S(2)}, u32[]{:S(2)}) collective-permute-start(f32[2,8,8,128]{3,2,1,0:T(8,128)S(1)} %get-tuple-element.31), channel_id=1, source_target_pairs={{0,16},{1,17},{2,18},{3,19},{4,20},{5,21},{6,22},{7,23},{8,24},{9,... | collective-permute-start | bytes 196616 | tf_op jit(solution)/shard_map/ppermute | solution.py:19
  230.5 6.4 %collective-permute-start.37 = (f32[2,8,8,128]{3,2,1,0:T(8,128)S(1)}, f32[2,8,8,128]{3,2,1,0:T(8,128)S(1)}, u32[]{:S(2)}, u32[]{:S(2)}) collective-permute-start(f32[2,8,8,128]{3,2,1,0:T(8,128)S(1)} %get-tuple-element.32), channel_id=1, source_target_pairs={{16,0},{17,1},{18,2},{19,3},{20,4},{21,5},{22,6},{23,7},{24,8},{25... | collective-permute-start | bytes 196616 | tf_op jit(solution)/shard_map/ppermute | solution.py:20
  237.2 5.9 %collective-permute-start.38 = (f32[12,2,8,128]{3,2,1,0:T(8,128)S(1)}, f32[12,2,8,128]{3,2,1,0:T(8,128)S(1)}, u32[]{:S(2)}, u32[]{:S(2)}) collective-permute-start(f32[12,2,8,128]{3,2,1,0:T(8,128)S(1)} %get-tuple-element.27), channel_id=1, source_target_pairs={{0,4},{4,8},{8,12},{1,5},{5,9},{9,13},{2,6},{6,10},{10,14},{3,7},{... | collective-permute-start | bytes 294920 | tf_op jit(solution)/shard_map/ppermute | solution.py:19
  239.1 5.8 %collective-permute-start.39 = (f32[12,2,8,128]{3,2,1,0:T(8,128)S(1)}, f32[12,2,8,128]{3,2,1,0:T(8,128)S(1)}, u32[]{:S(2)}, u32[]{:S(2)}) collective-permute-start(f32[12,2,8,128]{3,2,1,0:T(8,128)S(1)} %get-tuple-element.28), channel_id=1, source_target_pairs={{4,0},{8,4},{12,8},{5,1},{9,5},{13,9},{6,2},{10,6},{14,10},{7,3},{... | collective-permute-start | bytes 294920 | tf_op jit(solution)/shard_map/ppermute | solution.py:20
  245.2 7.0 %collective-permute-start.40 = (f32[12,12,2,128]{3,2,1,0:T(2,128)S(1)}, f32[12,12,2,128]{3,2,1,0:T(2,128)S(1)}, u32[]{:S(2)}, u32[]{:S(2)}) collective-permute-start(f32[12,12,2,128]{3,2,1,0:T(2,128)S(1)} %get-tuple-element.24), channel_id=1, source_target_pairs={{0,1},{1,2},{2,3},{4,5},{5,6},{6,7},{8,9},{9,10},{10,11},{12,13},{... | collective-permute-start | bytes 442376 | tf_op jit(solution)/shard_map/ppermute | solution.py:19
  247.1 7.0 %collective-permute-start.41 = (f32[12,12,2,128]{3,2,1,0:T(2,128)S(1)}, f32[12,12,2,128]{3,2,1,0:T(2,128)S(1)}, u32[]{:S(2)}, u32[]{:S(2)}) collective-permute-start(f32[12,12,2,128]{3,2,1,0:T(2,128)S(1)} %get-tuple-element.23), channel_id=1, source_target_pairs={{1,0},{2,1},{3,2},{5,4},{6,5},{7,6},{9,8},{10,9},{11,10},{13,12},{... | collective-permute-start | bytes 442376 | tf_op jit(solution)/shard_map/ppermute | solution.py:20
  254.5 1.6 copy-start.9
  256.2 2.1 copy-start.1
  258.7 20.7 %copy-start.4 = (f32[16,16,16,64]{3,2,1,0:T(8,128)}, f32[16,16,16,64]{3,2,1,0:T(8,128)S(1)}, u32[]{:S(2)}) copy-start(f32[16,16,16,64]{3,2,1,0:T(8,128)S(1)} %slice_add_fusion.16) | copy-start | bytes 3145732
  258.8 8.3 %collective-permute-start.42 = (f32[2,16,16,128]{3,2,1,0:T(8,128)S(1)}, f32[2,16,16,128]{3,2,1,0:T(8,128)S(1)}, u32[]{:S(2)}, u32[]{:S(2)}) collective-permute-start(f32[2,16,16,128]{3,2,1,0:T(8,128)S(1)} %get-tuple-element.20), channel_id=1, source_target_pairs={{0,16},{1,17},{2,18},{3,19},{4,20},{5,21},{6,22},{7,23},{8,24},{9,... | collective-permute-start | bytes 786440 | tf_op jit(solution)/shard_map/ppermute | solution.py:19
  260.1 8.4 %collective-permute-start.43 = (f32[2,16,16,128]{3,2,1,0:T(8,128)S(1)}, f32[2,16,16,128]{3,2,1,0:T(8,128)S(1)}, u32[]{:S(2)}, u32[]{:S(2)}) collective-permute-start(f32[2,16,16,128]{3,2,1,0:T(8,128)S(1)} %get-tuple-element.21), channel_id=1, source_target_pairs={{16,0},{17,1},{18,2},{19,3},{20,4},{21,5},{22,6},{23,7},{24,8},{25... | collective-permute-start | bytes 786440 | tf_op jit(solution)/shard_map/ppermute | solution.py:20
  269.3 8.4 %collective-permute-start.44 = (f32[20,2,16,128]{3,2,1,0:T(8,128)S(1)}, f32[20,2,16,128]{3,2,1,0:T(8,128)S(1)}, u32[]{:S(2)}, u32[]{:S(2)}) collective-permute-start(f32[20,2,16,128]{3,2,1,0:T(8,128)S(1)} %get-tuple-element.16), channel_id=1, source_target_pairs={{0,4},{4,8},{8,12},{1,5},{5,9},{9,13},{2,6},{6,10},{10,14},{3,7},{... | collective-permute-start | bytes 983048 | tf_op jit(solution)/shard_map/ppermute | solution.py:19
  271.2 8.2 %collective-permute-start.45 = (f32[20,2,16,128]{3,2,1,0:T(8,128)S(1)}, f32[20,2,16,128]{3,2,1,0:T(8,128)S(1)}, u32[]{:S(2)}, u32[]{:S(2)}) collective-permute-start(f32[20,2,16,128]{3,2,1,0:T(8,128)S(1)} %get-tuple-element.17), channel_id=1, source_target_pairs={{4,0},{8,4},{12,8},{5,1},{9,5},{13,9},{6,2},{10,6},{14,10},{7,3},{... | collective-permute-start | bytes 983048 | tf_op jit(solution)/shard_map/ppermute | solution.py:20
  281.3 10.2 %collective-permute-start.46 = (f32[20,20,2,128]{3,2,1,0:T(2,128)}, f32[20,20,2,128]{3,2,1,0:T(2,128)}, u32[]{:S(2)}, u32[]{:S(2)}) collective-permute-start(f32[20,20,2,128]{3,2,1,0:T(2,128)} %get-tuple-element.13), channel_id=1, source_target_pairs={{0,1},{1,2},{2,3},{4,5},{5,6},{6,7},{8,9},{9,10},{10,11},{12,13},{... | collective-permute-start | bytes 1228808 | tf_op jit(solution)/shard_map/ppermute | solution.py:19
  283.2 10.5 %collective-permute-start.47 = (f32[20,20,2,128]{3,2,1,0:T(2,128)}, f32[20,20,2,128]{3,2,1,0:T(2,128)}, u32[]{:S(2)}, u32[]{:S(2)}) collective-permute-start(f32[20,20,2,128]{3,2,1,0:T(2,128)} %get-tuple-element.12), channel_id=1, source_target_pairs={{1,0},{2,1},{3,2},{5,4},{6,5},{7,6},{9,8},{10,9},{11,10},{13,12},{... | collective-permute-start | bytes 1228808 | tf_op jit(solution)/shard_map/ppermute | solution.py:20
  290.9 7.3 %copy-start.5 = (f32[16,16,16,64]{3,2,1,0:T(8,128)S(1)}, f32[16,16,16,64]{3,2,1,0:T(8,128)}, u32[]{:S(2)}) copy-start(f32[16,16,16,64]{3,2,1,0:T(8,128)} %copy-done.4) | copy-start | bytes 3145732
  290.9 7.3 %copy-start.11 = (f32[18,18,18]{2,1,0:T(8,128)S(1)}, f32[18,18,18]{2,1,0:T(8,128)}, u32[]{:S(2)}) copy-start(f32[18,18,18]{2,1,0:T(8,128)} %copy-done.10) | copy-start | bytes 69988
  310.8 2.9 copy-start.6
  (3 other events, 3.5 us)
where the time goes:
time: 365 us; the launch traced here: 363 us
  starting transfers between devices  139 us (38%)
  blocking collectives  85.3 us (23%)
  waiting for transfers between devices  62.1 us (17%)
  other arithmetic  54.9 us (15%)
  local copies, waits for them, and re-layouts  14.3 us (4%)
  matrix products  5.15 us (1%)
    ppermute x24, starting transfers between devices, extended_2(): after = lax.ppermute(initial, axis, down)  94.3 us
    ppermute x24, starting transfers between devices, extended_2(): before = lax.ppermute(last, axis, up)  44.7 us
    psum x1, blocking collectives, local(): summed = lax.psum(partial_block, ('gx', 'gy', 'gz'))  43 us
    unnamed x1, blocking collectives  42.3 us
    ppermute x24, waiting for transfers between devices, extended_2(): after = lax.ppermute(initial, axis, down)  42.2 us
    mul x8, other arithmetic, double_sweep(): sweep_inner(extended[..., :count], source_wide, factor)  23.4 us
    ppermute x24, waiting for transfers between devices, extended_2(): before = lax.ppermute(last, axis, up)  19.9 us
    concatenate x24, other arithmetic, extended_2(): x = jnp.concatenate([before, x, after], axis=dim)  15.6 us
  transfers between devices with their start and end apart: 48, of which 37 were waited for; matrix products, arithmetic and copies ran while one was open for 1% of the time, Pallas kernels for 0%

commit v1 on v0

--- a/solution.py
+++ b/solution.py
@@ -134,7 +134,8 @@
         precision=lax.Precision.HIGHEST,
         preferred_element_type=jnp.float32,
     )
-    summed = lax.psum(partial_block, ("gx", "gy", "gz"))
+    parts = lax.all_gather(partial_block, ("gx", "gy", "gz"), axis=0, tiled=False)
+    summed = parts.sum(axis=0)
     total_cells = (
         cells_x
         * cells_y

time: 365 us -> 397 us (1.088)
  the two profiles are of different devices: /device:TPU:14 before, /device:TPU:0 now
where the time goes in v1:
time: 397 us; the launch traced here: 395 us
  waiting for transfers between devices  117 us (29%)
  blocking collectives  111 us (28%)
  starting transfers between devices  90.3 us (23%)
  other arithmetic  55 us (14%)
  local copies, waits for them, and re-layouts  14.5 us (4%)
  matrix products  5.15 us (1%)
    ppermute x24, waiting for transfers between devices, extended_2(): after = lax.ppermute(initial, axis, down)  98.7 us
    all_gather x1, blocking collectives, local(): lax.all_gather(partial_block, ('gx', 'gy', 'gz'), axis=0, tiled=False)  72.9 us
    ppermute x24, starting transfers between devices, extended_2(): before = lax.ppermute(last, axis, up)  58.9 us
    unnamed x1, blocking collectives  38.2 us
    ppermute x24, starting transfers between devices, extended_2(): after = lax.ppermute(initial, axis, down)  31.4 us
    mul x8, other arithmetic, double_sweep(): sweep_inner(extended[..., :count], source_wide, factor)  23.4 us
    ppermute x24, waiting for transfers between devices, extended_2(): before = lax.ppermute(last, axis, up)  18.4 us
    concatenate x24, other arithmetic, extended_2(): x = jnp.concatenate([before, x, after], axis=dim)  15.6 us
  transfers between devices with their start and end apart: 48, of which 35 were waited for; matrix products, arithmetic and copies ran while one was open for 1% of the time, Pallas kernels for 0%

profile of v1, /device:TPU:0, one launch (start us, length us, event | category | flops | bytes accessed | tf_op | source)
XLA Modules:
  0.0 394.9 jit_solution(17594652272153710157)
XLA Ops:
  0.6 1.7 reshape.351
  4.8 4.9 %collective-permute-start = (f32[2,16,16,128]{3,2,1,0:T(8,128)S(1)}, f32[2,16,16,128]{3,2,1,0:T(8,128)S(1)}, u32[]{:S(2)}, u32[]{:S(2)}) collective-permute-start(f32[2,16,16,128]{3,2,1,0:T(8,128)S(1)} %get-tuple-element.20), channel_id=1, source_target_pairs={{0,16},{1,17},{2,18},{3,19},{4,20},{5,21},{6,22},{7,23},{8,24},{9,... | collective-permute-start | bytes 786440 | tf_op jit(solution)/shard_map/ppermute | solution.py:19
  11.1 4.2 %collective-permute-done = f32[2,16,16,128]{3,2,1,0:T(8,128)S(1)} collective-permute-done((f32[2,16,16,128]{3,2,1,0:T(8,128)S(1)}, f32[2,16,16,128]{3,2,1,0:T(8,128)S(1)}, u32[]{:S(2)}, u32[]{:S(2)}) %collective-permute-start) | collective-permute-done | bytes 262176 | tf_op jit(solution)/shard_map/ppermute | solution.py:19
  15.2 4.1 %collective-permute-done.1 = f32[2,16,16,128]{3,2,1,0:T(8,128)S(1)} collective-permute-done((f32[2,16,16,128]{3,2,1,0:T(8,128)S(1)}, f32[2,16,16,128]{3,2,1,0:T(8,128)S(1)}, u32[]{:S(2)}, u32[]{:S(2)}) %collective-permute-start.1) | collective-permute-done | bytes 262176 | tf_op jit(solution)/shard_map/ppermute | solution.py:20
  19.4 2.2 fusion.55
  24.3 3.8 collective-permute-done.3
  29.2 3.5 collective-permute-start.4
  34.2 3.9 collective-permute-done.4
  38.1 4.7 %collective-permute-done.5 = f32[20,20,2,128]{3,2,1,0:T(2,128)S(1)} collective-permute-done((f32[20,20,2,128]{3,2,1,0:T(2,128)S(1)}, f32[20,20,2,128]{3,2,1,0:T(2,128)S(1)}, u32[]{:S(2)}, u32[]{:S(2)}) %collective-permute-start.5) | collective-permute-done | bytes 409632 | tf_op jit(solution)/shard_map/ppermute | solution.py:20
  42.8 3.2 fusion.5
  46.0 8.6 %fusion.23 = f32[18,18,18,64]{3,2,1,0:T(8,128)S(1)} fusion(f32[16,16,16,64]{3,2,1,0:T(8,128)S(1)} %reshape.351, f32[20,20,2,128]{3,2,1,0:T(2,128)S(1)} %collective-permute-done.4, f32[20,2,16,128]{3,2,1,0:T(8,128)S(1)} %collective-permute-done.3, f32[20,2,16,128]{3,2,1,0:T(8,128)S(1)} %collective-permute-done.2, ...), kind=kLoop, calls=%fused_computation.29 | loop fusion | flops 8584704 | bytes 14570272 | tf_op jit(solution)/shard_map/mul | solution.py:108
  54.7 2.6 fusion.63
  57.3 3.0 reduce_sum.61
  64.5 4.1 %collective-permute-done.7 = f32[2,8,8,128]{3,2,1,0:T(8,128)S(1)} collective-permute-done((f32[2,8,8,128]{3,2,1,0:T(8,128)S(1)}, f32[2,8,8,128]{3,2,1,0:T(8,128)S(1)}, u32[]{:S(2)}, u32[]{:S(2)}) %collective-permute-start.7) | collective-permute-done | bytes 65568 | tf_op jit(solution)/shard_map/ppermute | solution.py:20
  68.8 4.5 %collective-permute-start.8 = (f32[12,2,8,128]{3,2,1,0:T(8,128)S(1)}, f32[12,2,8,128]{3,2,1,0:T(8,128)S(1)}, u32[]{:S(2)}, u32[]{:S(2)}) collective-permute-start(f32[12,2,8,128]{3,2,1,0:T(8,128)S(1)} %get-tuple-element.27), channel_id=1, source_target_pairs={{0,4},{4,8},{8,12},{1,5},{5,9},{9,13},{2,6},{6,10},{10,14},{3,7},{... | collective-permute-start | bytes 294920 | tf_op jit(solution)/shard_map/ppermute | solution.py:19
  74.7 3.7 collective-permute-done.9
  78.6 3.5 collective-permute-start.10
  84.8 4.4 %collective-permute-done.11 = f32[12,12,2,128]{3,2,1,0:T(2,128)S(1)} collective-permute-done((f32[12,12,2,128]{3,2,1,0:T(2,128)S(1)}, f32[12,12,2,128]{3,2,1,0:T(2,128)S(1)}, u32[]{:S(2)}, u32[]{:S(2)}) %collective-permute-start.11) | collective-permute-done | bytes 147488 | tf_op jit(solution)/shard_map/ppermute | solution.py:20
  89.5 1.7 fusion.88
  91.7 1.6 collective-permute-start.12
  94.7 4.1 %collective-permute-done.13 = f32[2,4,4,128]{3,2,1,0:T(4,128)S(1)} collective-permute-done((f32[2,4,4,128]{3,2,1,0:T(4,128)S(1)}, f32[2,4,4,128]{3,2,1,0:T(4,128)S(1)}, u32[]{:S(2)}, u32[]{:S(2)}) %collective-permute-start.13) | collective-permute-done | bytes 16416 | tf_op jit(solution)/shard_map/ppermute | solution.py:20
  99.0 2.3 collective-permute-start.14
  102.6 4.0 %collective-permute-done.15 = f32[8,2,4,128]{3,2,1,0:T(4,128)S(1)} collective-permute-done((f32[8,2,4,128]{3,2,1,0:T(4,128)S(1)}, f32[8,2,4,128]{3,2,1,0:T(4,128)S(1)}, u32[]{:S(2)}, u32[]{:S(2)}) %collective-permute-start.15) | collective-permute-done | bytes 32800 | tf_op jit(solution)/shard_map/ppermute | solution.py:20
  106.8 3.5 collective-permute-start.16
  112.2 4.3 %collective-permute-done.17 = f32[8,8,2,128]{3,2,1,0:T(2,128)S(1)} collective-permute-done((f32[8,8,2,128]{3,2,1,0:T(2,128)S(1)}, f32[8,8,2,128]{3,2,1,0:T(2,128)S(1)}, u32[]{:S(2)}, u32[]{:S(2)}) %collective-permute-start.17) | collective-permute-done | bytes 65568 | tf_op jit(solution)/shard_map/ppermute | solution.py:20
  116.9 1.6 collective-permute-start.18
  120.6 3.5 collective-permute-done.19
  124.1 1.7 collective-permute-start.20
  127.1 4.1 %collective-permute-done.21 = f32[6,2,2,128]{3,2,1,0:T(2,128)S(1)} collective-permute-done((f32[6,2,2,128]{3,2,1,0:T(2,128)S(1)}, f32[6,2,2,128]{3,2,1,0:T(2,128)S(1)}, u32[]{:S(2)}, u32[]{:S(2)}) %collective-permute-start.21) | collective-permute-done | bytes 12320 | tf_op jit(solution)/shard_map/ppermute | solution.py:20
  131.9 1.9 collective-permute-start.22
  135.8 4.2 %collective-permute-done.23 = f32[6,6,2,128]{3,2,1,0:T(2,128)} collective-permute-done((f32[6,6,2,128]{3,2,1,0:T(2,128)}, f32[6,6,2,128]{3,2,1,0:T(2,128)}, u32[]{:S(2)}, u32[]{:S(2)}) %collective-permute-start.23) | collective-permute-done | bytes 36896 | tf_op jit(solution)/shard_map/ppermute | solution.py:20
  142.5 38.2 %all-reduce.11 = f32[2048]{0:T(1024)S(1)} all-reduce(f32[2048]{0:T(1024)S(1)} %multiply_dynamic-update-slice_fusion), channel_id=2, replica_groups=mesh['gx'=2,'gy'=4,'gz'=4] {'gx','gy','gz'}, use_global_device_ids=true, to_apply=%add.11 | all-reduce | flops 2048 | bytes 16384
  181.9 4.2 %collective-permute-start.24 = (f32[2,2,2,128]{3,2,1,0:T(2,128)S(1)}, f32[2,2,2,128]{3,2,1,0:T(2,128)S(1)}, u32[]{:S(2)}, u32[]{:S(2)}) collective-permute-start(f32[2,2,2,128]{3,2,1,0:T(2,128)S(1)} %pad_maximum_fusion.47), channel_id=1, source_target_pairs={{0,16},{1,17},{2,18},{3,19},{4,20},{5,21},{6,22},{7,23},{8,24},{9,... | collective-permute-start | bytes 12296 | tf_op jit(solution)/shard_map/ppermute | solution.py:19
  187.4 4.2 %collective-permute-done.25 = f32[2,2,2,128]{3,2,1,0:T(2,128)S(1)} collective-permute-done((f32[2,2,2,128]{3,2,1,0:T(2,128)S(1)}, f32[2,2,2,128]{3,2,1,0:T(2,128)S(1)}, u32[]{:S(2)}, u32[]{:S(2)}) %collective-permute-start.25) | collective-permute-done | bytes 4128 | tf_op jit(solution)/shard_map/ppermute | solution.py:20
  194.3 3.9 collective-permute-done.27
  198.2 3.9 collective-permute-start.28
  203.8 4.2 %collective-permute-done.29 = f32[6,6,2,128]{3,2,1,0:T(2,128)S(1)} collective-permute-done((f32[6,6,2,128]{3,2,1,0:T(2,128)S(1)}, f32[6,6,2,128]{3,2,1,0:T(2,128)S(1)}, u32[]{:S(2)}, u32[]{:S(2)}) %collective-permute-start.29) | collective-permute-done | bytes 36896 | tf_op jit(solution)/shard_map/ppermute | solution.py:20
  208.4 1.7 collective-permute-start.30
  211.5 4.2 %collective-permute-done.31 = f32[2,4,4,128]{3,2,1,0:T(4,128)S(1)} collective-permute-done((f32[2,4,4,128]{3,2,1,0:T(4,128)S(1)}, f32[2,4,4,128]{3,2,1,0:T(4,128)S(1)}, u32[]{:S(2)}, u32[]{:S(2)}) %collective-permute-start.31) | collective-permute-done | bytes 16416 | tf_op jit(solution)/shard_map/ppermute | solution.py:20
  218.6 4.2 %collective-permute-done.33 = f32[8,2,4,128]{3,2,1,0:T(4,128)S(1)} collective-permute-done((f32[8,2,4,128]{3,2,1,0:T(4,128)S(1)}, f32[8,2,4,128]{3,2,1,0:T(4,128)S(1)}, u32[]{:S(2)}, u32[]{:S(2)}) %collective-permute-start.33) | collective-permute-done | bytes 32800 | tf_op jit(solution)/shard_map/ppermute | solution.py:20
  222.9 2.6 collective-permute-start.34
  227.4 4.3 %collective-permute-done.35 = f32[8,8,2,128]{3,2,1,0:T(2,128)S(1)} collective-permute-done((f32[8,8,2,128]{3,2,1,0:T(2,128)S(1)}, f32[8,8,2,128]{3,2,1,0:T(2,128)S(1)}, u32[]{:S(2)}, u32[]{:S(2)}) %collective-permute-start.35) | collective-permute-done | bytes 65568 | tf_op jit(solution)/shard_map/ppermute | solution.py:20
  233.1 1.6 collective-permute-start.36
  236.9 4.6 %collective-permute-done.37 = f32[2,8,8,128]{3,2,1,0:T(8,128)S(1)} collective-permute-done((f32[2,8,8,128]{3,2,1,0:T(8,128)S(1)}, f32[2,8,8,128]{3,2,1,0:T(8,128)S(1)}, u32[]{:S(2)}, u32[]{:S(2)}) %collective-permute-start.37) | collective-permute-done | bytes 65568 | tf_op jit(solution)/shard_map/ppermute | solution.py:20
  241.7 2.0 collective-permute-start.38
  245.0 3.3 collective-permute-done.39
  248.5 1.9 collective-permute-start.40
  253.1 4.4 %collective-permute-done.41 = f32[12,12,2,128]{3,2,1,0:T(2,128)S(1)} collective-permute-done((f32[12,12,2,128]{3,2,1,0:T(2,128)S(1)}, f32[12,12,2,128]{3,2,1,0:T(2,128)S(1)}, u32[]{:S(2)}, u32[]{:S(2)}) %collective-permute-start.41) | collective-permute-done | bytes 147488 | tf_op jit(solution)/shard_map/ppermute | solution.py:20
  257.8 1.6 fusion.101
  262.2 1.6 collective-permute-start.42
  265.1 4.5 %collective-permute-done.42 = f32[2,16,16,128]{3,2,1,0:T(8,128)S(1)} collective-permute-done((f32[2,16,16,128]{3,2,1,0:T(8,128)S(1)}, f32[2,16,16,128]{3,2,1,0:T(8,128)S(1)}, u32[]{:S(2)}, u32[]{:S(2)}) %collective-permute-start.42) | collective-permute-done | bytes 262176 | tf_op jit(solution)/shard_map/ppermute | solution.py:19
  269.6 4.7 %collective-permute-done.43 = f32[2,16,16,128]{3,2,1,0:T(8,128)S(1)} collective-permute-done((f32[2,16,16,128]{3,2,1,0:T(8,128)S(1)}, f32[2,16,16,128]{3,2,1,0:T(8,128)S(1)}, u32[]{:S(2)}, u32[]{:S(2)}) %collective-permute-start.43) | collective-permute-done | bytes 262176 | tf_op jit(solution)/shard_map/ppermute | solution.py:20
  275.0 2.3 collective-permute-start.44
  278.6 2.2 collective-permute-done.45
  282.7 2.7 collective-permute-start.46
  285.4 1.5 collective-permute-start.47
  286.9 2.8 reshape_reshape.3
  290.4 5.4 %collective-permute-done.47 = f32[20,20,2,128]{3,2,1,0:T(2,128)} collective-permute-done((f32[20,20,2,128]{3,2,1,0:T(2,128)}, f32[20,20,2,128]{3,2,1,0:T(2,128)}, u32[]{:S(2)}, u32[]{:S(2)}) %collective-permute-start.47) | collective-permute-done | bytes 409632 | tf_op jit(solution)/shard_map/ppermute | solution.py:20
  295.8 4.6 %fusion.11 = f32[20,20,20,128]{3,2,1,0:T(8,128)S(1)} fusion(f32[16,16,16,64]{3,2,1,0:T(8,128)S(1)} %reshape.351, f32[20,20,2,128]{3,2,1,0:T(2,128)} %collective-permute-done.47, f32[20,2,16,128]{3,2,1,0:T(8,128)S(1)} %collective-permute-done.45, f32[2,16,16,128]{3,2,1,0:T(8,128)S(1)} %collective-permute-done.43, f32[16,16,16,64]{3,2,1,0:T(8,128)} %copy-done.4, ...), kind=kLoop, calls=%fused_computation.13 | loop fusion | flops 7168000 | bytes 8192000 | tf_op jit(solution)/shard_map/concatenate | solution.py:21
  300.4 9.5 %fusion.35 = f32[18,18,18,64]{3,2,1,0:T(8,128)S(1)} fusion(f32[16,16,16,64]{3,2,1,0:T(8,128)S(1)} %reshape.351, f32[20,20,2,128]{3,2,1,0:T(2,128)} %collective-permute-done.46, f32[20,2,16,128]{3,2,1,0:T(8,128)S(1)} %collective-permute-done.45, f32[20,2,16,128]{3,2,1,0:T(8,128)S(1)} %collective-permute-done.44, ...), kind=kLoop, calls=%fused_computation.41 | loop fusion | flops 8584704 | bytes 14570272 | tf_op jit(solution)/shard_map/mul | solution.py:108
  309.9 3.1 fusion.61
  313.0 2.9 reshape.365
  315.9 5.2 %convolution_bitcast_fusion = f32[64,64]{0,1:T(8,128)S(1)} fusion(f32[4096,64]{1,0:T(8,128)S(1)} %bitcast.74, f32[4096,64]{1,0:T(8,128)} %reshape_reshape.3), kind=kOutput, calls=%fused_computation.108 | convolution fusion | flops 201326592 | bytes 2113536 | tf_op jit(solution)/shard_map/dot_general | solution.py:131
  321.1 72.9 %all-gather.1 = f32[2048,64]{1,0:T(8,128)S(1)} all-gather(f32[64,64]{1,0:T(8,128)S(1)} %copy.6), channel_id=3, replica_groups=mesh['gx'=2,'gy'=4,'gz'=4] {'gx','gy','gz'}, dimensions={0}, use_global_device_ids=true | all-gather | bytes 540672 | tf_op jit(solution)/shard_map/all_gather | solution.py:137
  (198 shorter events, 63.3 us)
Async XLA Ops:
  4.8 10.4 %collective-permute-start = (f32[2,16,16,128]{3,2,1,0:T(8,128)S(1)}, f32[2,16,16,128]{3,2,1,0:T(8,128)S(1)}, u32[]{:S(2)}, u32[]{:S(2)}) collective-permute-start(f32[2,16,16,128]{3,2,1,0:T(8,128)S(1)} %get-tuple-element.20), channel_id=1, source_target_pairs={{0,16},{1,17},{2,18},{3,19},{4,20},{5,21},{6,22},{7,23},{8,24},{9,... | collective-permute-start | bytes 786440 | tf_op jit(solution)/shard_map/ppermute | solution.py:19
  9.7 9.7 %collective-permute-start.1 = (f32[2,16,16,128]{3,2,1,0:T(8,128)S(1)}, f32[2,16,16,128]{3,2,1,0:T(8,128)S(1)}, u32[]{:S(2)}, u32[]{:S(2)}) collective-permute-start(f32[2,16,16,128]{3,2,1,0:T(8,128)S(1)} %get-tuple-element.8), channel_id=1, source_target_pairs={{16,0},{17,1},{18,2},{19,3},{20,4},{21,5},{22,6},{23,7},{24,8},{25... | collective-permute-start | bytes 786440 | tf_op jit(solution)/shard_map/ppermute | solution.py:20
  11.1 17.1 %copy-start.3 = (f32[16,16,16,64]{3,2,1,0:T(8,128)S(1)}, f32[16,16,16,64]{3,2,1,0:T(8,128)}, u32[]{:S(2)}) copy-start(f32[16,16,16,64]{3,2,1,0:T(8,128)} %copy-done.2) | copy-start | bytes 3145732
  21.6 2.7 collective-permute-start.2
  22.9 5.2 %collective-permute-start.3 = (f32[20,2,16,128]{3,2,1,0:T(8,128)S(1)}, f32[20,2,16,128]{3,2,1,0:T(8,128)S(1)}, u32[]{:S(2)}, u32[]{:S(2)}) collective-permute-start(f32[20,2,16,128]{3,2,1,0:T(8,128)S(1)} %get-tuple-element.17), channel_id=1, source_target_pairs={{4,0},{8,4},{12,8},{5,1},{9,5},{13,9},{6,2},{10,6},{14,10},{7,3},{... | collective-permute-start | bytes 983048 | tf_op jit(solution)/shard_map/ppermute | solution.py:20
  29.2 8.9 %collective-permute-start.4 = (f32[20,20,2,128]{3,2,1,0:T(2,128)S(1)}, f32[20,20,2,128]{3,2,1,0:T(2,128)S(1)}, u32[]{:S(2)}, u32[]{:S(2)}) collective-permute-start(f32[20,20,2,128]{3,2,1,0:T(2,128)S(1)} %get-tuple-element.13), channel_id=1, source_target_pairs={{0,1},{1,2},{2,3},{4,5},{5,6},{6,7},{8,9},{9,10},{10,11},{12,13},{... | collective-permute-start | bytes 1228808 | tf_op jit(solution)/shard_map/ppermute | solution.py:19
  32.7 10.1 %collective-permute-start.5 = (f32[20,20,2,128]{3,2,1,0:T(2,128)S(1)}, f32[20,20,2,128]{3,2,1,0:T(2,128)S(1)}, u32[]{:S(2)}, u32[]{:S(2)}) collective-permute-start(f32[20,20,2,128]{3,2,1,0:T(2,128)S(1)} %get-tuple-element.12), channel_id=1, source_target_pairs={{1,0},{2,1},{3,2},{5,4},{6,5},{7,6},{9,8},{10,9},{11,10},{13,12},{... | collective-permute-start | bytes 1228808 | tf_op jit(solution)/shard_map/ppermute | solution.py:20
  34.2 11.8 %copy-start.10 = (f32[18,18,18]{2,1,0:T(8,128)}, f32[18,18,18]{2,1,0:T(8,128)S(1)}, u32[]{:S(2)}) copy-start(f32[18,18,18]{2,1,0:T(8,128)S(1)} %and_convert_fusion) | copy-start | bytes 69988
  54.6 2.6 copy-start
  60.3 28.9 %copy-start.7 = (f32[8,8,8,64]{3,2,1,0:T(8,128)}, f32[8,8,8,64]{3,2,1,0:T(8,128)S(1)}, u32[]{:S(2)}) copy-start(f32[8,8,8,64]{3,2,1,0:T(8,128)S(1)} %reduce_sum.61) | copy-start | bytes 393220
  61.1 3.5 collective-permute-start.6
  62.5 6.2 %collective-permute-start.7 = (f32[2,8,8,128]{3,2,1,0:T(8,128)S(1)}, f32[2,8,8,128]{3,2,1,0:T(8,128)S(1)}, u32[]{:S(2)}, u32[]{:S(2)}) collective-permute-start(f32[2,8,8,128]{3,2,1,0:T(8,128)S(1)} %get-tuple-element.6), channel_id=1, source_target_pairs={{16,0},{17,1},{18,2},{19,3},{20,4},{21,5},{22,6},{23,7},{24,8},{25... | collective-permute-start | bytes 196616 | tf_op jit(solution)/shard_map/ppermute | solution.py:20
  64.5 25.0 %copy-start.14 = (f32[10,10,10]{2,1,0:T(8,128)S(1)}, f32[10,10,10]{2,1,0:T(8,128)}, u32[]{:S(2)}) copy-start(f32[10,10,10]{2,1,0:T(8,128)} %and_convert_fusion.1) | copy-start | bytes 12004
  68.7 20.5 %copy-start.12 = (f32[2,8,8,128]{3,2,1,0:T(8,128)}, f32[2,8,8,128]{3,2,1,0:T(8,128)S(1)}, u32[]{:S(2)}) copy-start(f32[2,8,8,128]{3,2,1,0:T(8,128)S(1)} %collective-permute-done.7) | copy-start | bytes 196612
  68.8 5.9 %collective-permute-start.8 = (f32[12,2,8,128]{3,2,1,0:T(8,128)S(1)}, f32[12,2,8,128]{3,2,1,0:T(8,128)S(1)}, u32[]{:S(2)}, u32[]{:S(2)}) collective-permute-start(f32[12,2,8,128]{3,2,1,0:T(8,128)S(1)} %get-tuple-element.27), channel_id=1, source_target_pairs={{0,4},{4,8},{8,12},{1,5},{5,9},{9,13},{2,6},{6,10},{10,14},{3,7},{... | collective-permute-start | bytes 294920 | tf_op jit(solution)/shard_map/ppermute | solution.py:19
  73.4 5.0 %collective-permute-start.9 = (f32[12,2,8,128]{3,2,1,0:T(8,128)S(1)}, f32[12,2,8,128]{3,2,1,0:T(8,128)S(1)}, u32[]{:S(2)}, u32[]{:S(2)}) collective-permute-start(f32[12,2,8,128]{3,2,1,0:T(8,128)S(1)} %get-tuple-element.28), channel_id=1, source_target_pairs={{4,0},{8,4},{12,8},{5,1},{9,5},{13,9},{6,2},{10,6},{14,10},{7,3},{... | collective-permute-start | bytes 294920 | tf_op jit(solution)/shard_map/ppermute | solution.py:20
  78.6 6.1 %collective-permute-start.10 = (f32[12,12,2,128]{3,2,1,0:T(2,128)S(1)}, f32[12,12,2,128]{3,2,1,0:T(2,128)S(1)}, u32[]{:S(2)}, u32[]{:S(2)}) collective-permute-start(f32[12,12,2,128]{3,2,1,0:T(2,128)S(1)} %get-tuple-element.24), channel_id=1, source_target_pairs={{0,1},{1,2},{2,3},{4,5},{5,6},{6,7},{8,9},{9,10},{10,11},{12,13},{... | collective-permute-start | bytes 442376 | tf_op jit(solution)/shard_map/ppermute | solution.py:19
  82.1 7.0 %collective-permute-start.11 = (f32[12,12,2,128]{3,2,1,0:T(2,128)S(1)}, f32[12,12,2,128]{3,2,1,0:T(2,128)S(1)}, u32[]{:S(2)}, u32[]{:S(2)}) collective-permute-start(f32[12,12,2,128]{3,2,1,0:T(2,128)S(1)} %get-tuple-element.23), channel_id=1, source_target_pairs={{1,0},{2,1},{3,2},{5,4},{6,5},{7,6},{9,8},{10,9},{11,10},{13,12},{... | collective-permute-start | bytes 442376 | tf_op jit(solution)/shard_map/ppermute | solution.py:20
  89.5 1.7 copy-start.8
  91.7 3.1 collective-permute-start.12
  93.2 5.6 %collective-permute-start.13 = (f32[2,4,4,128]{3,2,1,0:T(4,128)S(1)}, f32[2,4,4,128]{3,2,1,0:T(4,128)S(1)}, u32[]{:S(2)}, u32[]{:S(2)}) collective-permute-start(f32[2,4,4,128]{3,2,1,0:T(4,128)S(1)} %get-tuple-element.45), channel_id=1, source_target_pairs={{16,0},{17,1},{18,2},{19,3},{20,4},{21,5},{22,6},{23,7},{24,8},{25... | collective-permute-start | bytes 49160 | tf_op jit(solution)/shard_map/ppermute | solution.py:20
  99.0 3.7 collective-permute-start.14
  101.3 5.4 %collective-permute-start.15 = (f32[8,2,4,128]{3,2,1,0:T(4,128)S(1)}, f32[8,2,4,128]{3,2,1,0:T(4,128)S(1)}, u32[]{:S(2)}, u32[]{:S(2)}) collective-permute-start(f32[8,2,4,128]{3,2,1,0:T(4,128)S(1)} %get-tuple-element.43), channel_id=1, source_target_pairs={{4,0},{8,4},{12,8},{5,1},{9,5},{13,9},{6,2},{10,6},{14,10},{7,3},{... | collective-permute-start | bytes 98312 | tf_op jit(solution)/shard_map/ppermute | solution.py:20
  102.6 32.6 %copy-start.17 = (f32[6,6,6]{2,1,0:T(8,128)}, f32[6,6,6]{2,1,0:T(8,128)S(1)}, u32[]{:S(2)}) copy-start(f32[6,6,6]{2,1,0:T(8,128)S(1)} %and_convert_fusion.2) | copy-start | bytes 2596
  106.8 5.4 %collective-permute-start.16 = (f32[8,8,2,128]{3,2,1,0:T(2,128)S(1)}, f32[8,8,2,128]{3,2,1,0:T(2,128)S(1)}, u32[]{:S(2)}, u32[]{:S(2)}) collective-permute-start(f32[8,8,2,128]{3,2,1,0:T(2,128)S(1)} %get-tuple-element.37), channel_id=1, source_target_pairs={{0,1},{1,2},{2,3},{4,5},{5,6},{6,7},{8,9},{9,10},{10,11},{12,13},{... | collective-permute-start | bytes 196616 | tf_op jit(solution)/shard_map/ppermute | solution.py:19
  110.3 6.2 %collective-permute-start.17 = (f32[8,8,2,128]{3,2,1,0:T(2,128)S(1)}, f32[8,8,2,128]{3,2,1,0:T(2,128)S(1)}, u32[]{:S(2)}, u32[]{:S(2)}) collective-permute-start(f32[8,8,2,128]{3,2,1,0:T(2,128)S(1)} %get-tuple-element.36), channel_id=1, source_target_pairs={{1,0},{2,1},{3,2},{5,4},{6,5},{7,6},{9,8},{10,9},{11,10},{13,12},{... | collective-permute-start | bytes 196616 | tf_op jit(solution)/shard_map/ppermute | solution.py:20
  116.9 3.7 collective-permute-start.18
  118.6 5.5 %collective-permute-start.19 = (f32[2,2,2,128]{3,2,1,0:T(2,128)S(1)}, f32[2,2,2,128]{3,2,1,0:T(2,128)S(1)}, u32[]{:S(2)}, u32[]{:S(2)}) collective-permute-start(f32[2,2,2,128]{3,2,1,0:T(2,128)S(1)} %pad_maximum_fusion.46), channel_id=1, source_target_pairs={{16,0},{17,1},{18,2},{19,3},{20,4},{21,5},{22,6},{23,7},{24,8},{25... | collective-permute-start | bytes 12296 | tf_op jit(solution)/shard_map/ppermute | solution.py:20
  124.1 3.0 collective-permute-start.20
  125.8 5.4 %collective-permute-start.21 = (f32[6,2,2,128]{3,2,1,0:T(2,128)S(1)}, f32[6,2,2,128]{3,2,1,0:T(2,128)S(1)}, u32[]{:S(2)}, u32[]{:S(2)}) collective-permute-start(f32[6,2,2,128]{3,2,1,0:T(2,128)S(1)} %fusion.281), channel_id=1, source_target_pairs={{4,0},{8,4},{12,8},{5,1},{9,5},{13,9},{6,2},{10,6},{14,10},{7,3},{... | collective-permute-start | bytes 36872 | tf_op jit(solution)/shard_map/ppermute | solution.py:20
  131.9 3.8 collective-permute-start.22
  133.9 6.2 %collective-permute-start.23 = (f32[6,6,2,128]{3,2,1,0:T(2,128)}, f32[6,6,2,128]{3,2,1,0:T(2,128)}, u32[]{:S(2)}, u32[]{:S(2)}) collective-permute-start(f32[6,6,2,128]{3,2,1,0:T(2,128)} %fusion.211), channel_id=1, source_target_pairs={{1,0},{2,1},{3,2},{5,4},{6,5},{7,6},{9,8},{10,9},{11,10},{13,12},{... | collective-permute-start | bytes 110600 | tf_op jit(solution)/shard_map/ppermute | solution.py:20
  135.2 97.7 %copy-start.16 = (f32[2,8,8,128]{3,2,1,0:T(8,128)S(1)}, f32[2,8,8,128]{3,2,1,0:T(8,128)}, u32[]{:S(2)}) copy-start(f32[2,8,8,128]{3,2,1,0:T(8,128)} %get-tuple-element.7) | copy-start | bytes 196612
  181.9 5.5 %collective-permute-start.24 = (f32[2,2,2,128]{3,2,1,0:T(2,128)S(1)}, f32[2,2,2,128]{3,2,1,0:T(2,128)S(1)}, u32[]{:S(2)}, u32[]{:S(2)}) collective-permute-start(f32[2,2,2,128]{3,2,1,0:T(2,128)S(1)} %pad_maximum_fusion.47), channel_id=1, source_target_pairs={{0,16},{1,17},{2,18},{3,19},{4,20},{5,21},{6,22},{7,23},{8,24},{9,... | collective-permute-start | bytes 12296 | tf_op jit(solution)/shard_map/ppermute | solution.py:19
  186.1 5.5 %collective-permute-start.25 = (f32[2,2,2,128]{3,2,1,0:T(2,128)S(1)}, f32[2,2,2,128]{3,2,1,0:T(2,128)S(1)}, u32[]{:S(2)}, u32[]{:S(2)}) collective-permute-start(f32[2,2,2,128]{3,2,1,0:T(2,128)S(1)} %pad_maximum_fusion.47), channel_id=1, source_target_pairs={{16,0},{17,1},{18,2},{19,3},{20,4},{21,5},{22,6},{23,7},{24,8},{25... | collective-permute-start | bytes 12296 | tf_op jit(solution)/shard_map/ppermute | solution.py:20
  191.7 2.6 collective-permute-start.26
  192.9 5.2 %collective-permute-start.27 = (f32[6,2,2,128]{3,2,1,0:T(2,128)S(1)}, f32[6,2,2,128]{3,2,1,0:T(2,128)S(1)}, u32[]{:S(2)}, u32[]{:S(2)}) collective-permute-start(f32[6,2,2,128]{3,2,1,0:T(2,128)S(1)} %fusion.283), channel_id=1, source_target_pairs={{4,0},{8,4},{12,8},{5,1},{9,5},{13,9},{6,2},{10,6},{14,10},{7,3},{... | collective-permute-start | bytes 36872 | tf_op jit(solution)/shard_map/ppermute | solution.py:20
  198.2 5.5 %collective-permute-start.28 = (f32[6,6,2,128]{3,2,1,0:T(2,128)S(1)}, f32[6,6,2,128]{3,2,1,0:T(2,128)S(1)}, u32[]{:S(2)}, u32[]{:S(2)}) collective-permute-start(f32[6,6,2,128]{3,2,1,0:T(2,128)S(1)} %fusion.215), channel_id=1, source_target_pairs={{0,1},{1,2},{2,3},{4,5},{5,6},{6,7},{8,9},{9,10},{10,11},{12,13},{... | collective-permute-start | bytes 110600 | tf_op jit(solution)/shard_map/ppermute | solution.py:19
  202.1 5.9 %collective-permute-start.29 = (f32[6,6,2,128]{3,2,1,0:T(2,128)S(1)}, f32[6,6,2,128]{3,2,1,0:T(2,128)S(1)}, u32[]{:S(2)}, u32[]{:S(2)}) collective-permute-start(f32[6,6,2,128]{3,2,1,0:T(2,128)S(1)} %fusion.215), channel_id=1, source_target_pairs={{1,0},{2,1},{3,2},{5,4},{6,5},{7,6},{9,8},{10,9},{11,10},{13,12},{... | collective-permute-start | bytes 110600 | tf_op jit(solution)/shard_map/ppermute | solution.py:20
  208.4 3.1 collective-permute-start.30
  210.0 5.6 %collective-permute-start.31 = (f32[2,4,4,128]{3,2,1,0:T(4,128)S(1)}, f32[2,4,4,128]{3,2,1,0:T(4,128)S(1)}, u32[]{:S(2)}, u32[]{:S(2)}) collective-permute-start(f32[2,4,4,128]{3,2,1,0:T(4,128)S(1)} %get-tuple-element.41), channel_id=1, source_target_pairs={{16,0},{17,1},{18,2},{19,3},{20,4},{21,5},{22,6},{23,7},{24,8},{25... | collective-permute-start | bytes 49160 | tf_op jit(solution)/shard_map/ppermute | solution.py:20
  215.8 2.8 collective-permute-start.32
  217.3 5.5 %collective-permute-start.33 = (f32[8,2,4,128]{3,2,1,0:T(4,128)S(1)}, f32[8,2,4,128]{3,2,1,0:T(4,128)S(1)}, u32[]{:S(2)}, u32[]{:S(2)}) collective-permute-start(f32[8,2,4,128]{3,2,1,0:T(4,128)S(1)} %get-tuple-element.39), channel_id=1, source_target_pairs={{4,0},{8,4},{12,8},{5,1},{9,5},{13,9},{6,2},{10,6},{14,10},{7,3},{... | collective-permute-start | bytes 98312 | tf_op jit(solution)/shard_map/ppermute | solution.py:20
  222.9 4.5 %collective-permute-start.34 = (f32[8,8,2,128]{3,2,1,0:T(2,128)S(1)}, f32[8,8,2,128]{3,2,1,0:T(2,128)S(1)}, u32[]{:S(2)}, u32[]{:S(2)}) collective-permute-start(f32[8,8,2,128]{3,2,1,0:T(2,128)S(1)} %get-tuple-element.35), channel_id=1, source_target_pairs={{0,1},{1,2},{2,3},{4,5},{5,6},{6,7},{8,9},{9,10},{10,11},{12,13},{... | collective-permute-start | bytes 196616 | tf_op jit(solution)/shard_map/ppermute | solution.py:19
  225.5 6.2 %collective-permute-start.35 = (f32[8,8,2,128]{3,2,1,0:T(2,128)S(1)}, f32[8,8,2,128]{3,2,1,0:T(2,128)S(1)}, u32[]{:S(2)}, u32[]{:S(2)}) collective-permute-start(f32[8,8,2,128]{3,2,1,0:T(2,128)S(1)} %get-tuple-element.34), channel_id=1, source_target_pairs={{1,0},{2,1},{3,2},{5,4},{6,5},{7,6},{9,8},{10,9},{11,10},{13,12},{... | collective-permute-start | bytes 196616 | tf_op jit(solution)/shard_map/ppermute | solution.py:20
  232.9 24.9 %copy-start.15 = (f32[10,10,10]{2,1,0:T(8,128)S(1)}, f32[10,10,10]{2,1,0:T(8,128)}, u32[]{:S(2)}) copy-start(f32[10,10,10]{2,1,0:T(8,128)} %and_convert_fusion.1) | copy-start | bytes 12004
  233.1 3.9 collective-permute-start.36
  234.7 6.8 %collective-permute-start.37 = (f32[2,8,8,128]{3,2,1,0:T(8,128)S(1)}, f32[2,8,8,128]{3,2,1,0:T(8,128)S(1)}, u32[]{:S(2)}, u32[]{:S(2)}) collective-permute-start(f32[2,8,8,128]{3,2,1,0:T(8,128)S(1)} %get-tuple-element.30), channel_id=1, source_target_pairs={{16,0},{17,1},{18,2},{19,3},{20,4},{21,5},{22,6},{23,7},{24,8},{25... | collective-permute-start | bytes 196616 | tf_op jit(solution)/shard_map/ppermute | solution.py:20
  241.7 3.3 collective-permute-start.38
  243.6 4.6 %collective-permute-start.39 = (f32[12,2,8,128]{3,2,1,0:T(8,128)S(1)}, f32[12,2,8,128]{3,2,1,0:T(8,128)S(1)}, u32[]{:S(2)}, u32[]{:S(2)}) collective-permute-start(f32[12,2,8,128]{3,2,1,0:T(8,128)S(1)} %get-tuple-element.26), channel_id=1, source_target_pairs={{4,0},{8,4},{12,8},{5,1},{9,5},{13,9},{6,2},{10,6},{14,10},{7,3},{... | collective-permute-start | bytes 294920 | tf_op jit(solution)/shard_map/ppermute | solution.py:20
  248.5 4.6 %collective-permute-start.40 = (f32[12,12,2,128]{3,2,1,0:T(2,128)S(1)}, f32[12,12,2,128]{3,2,1,0:T(2,128)S(1)}, u32[]{:S(2)}, u32[]{:S(2)}) collective-permute-start(f32[12,12,2,128]{3,2,1,0:T(2,128)S(1)} %get-tuple-element.22), channel_id=1, source_target_pairs={{0,1},{1,2},{2,3},{4,5},{5,6},{6,7},{8,9},{9,10},{10,11},{12,13},{... | collective-permute-start | bytes 442376 | tf_op jit(solution)/shard_map/ppermute | solution.py:19
  250.4 7.0 %collective-permute-start.41 = (f32[12,12,2,128]{3,2,1,0:T(2,128)S(1)}, f32[12,12,2,128]{3,2,1,0:T(2,128)S(1)}, u32[]{:S(2)}, u32[]{:S(2)}) collective-permute-start(f32[12,12,2,128]{3,2,1,0:T(2,128)S(1)} %get-tuple-element.21), channel_id=1, source_target_pairs={{1,0},{2,1},{3,2},{5,4},{6,5},{7,6},{9,8},{10,9},{11,10},{13,12},{... | collective-permute-start | bytes 442376 | tf_op jit(solution)/shard_map/ppermute | solution.py:20
  257.8 1.6 copy-start.9
  259.6 2.1 copy-start.1
  262.0 18.8 %copy-start.4 = (f32[16,16,16,64]{3,2,1,0:T(8,128)}, f32[16,16,16,64]{3,2,1,0:T(8,128)S(1)}, u32[]{:S(2)}) copy-start(f32[16,16,16,64]{3,2,1,0:T(8,128)S(1)} %slice_add_fusion.16) | copy-start | bytes 3145732
  262.2 7.4 %collective-permute-start.42 = (f32[2,16,16,128]{3,2,1,0:T(8,128)S(1)}, f32[2,16,16,128]{3,2,1,0:T(8,128)S(1)}, u32[]{:S(2)}, u32[]{:S(2)}) collective-permute-start(f32[2,16,16,128]{3,2,1,0:T(8,128)S(1)} %get-tuple-element.18), channel_id=1, source_target_pairs={{0,16},{1,17},{2,18},{3,19},{4,20},{5,21},{6,22},{7,23},{8,24},{9,... | collective-permute-start | bytes 786440 | tf_op jit(solution)/shard_map/ppermute | solution.py:19
  263.8 10.5 %collective-permute-start.43 = (f32[2,16,16,128]{3,2,1,0:T(8,128)S(1)}, f32[2,16,16,128]{3,2,1,0:T(8,128)S(1)}, u32[]{:S(2)}, u32[]{:S(2)}) collective-permute-start(f32[2,16,16,128]{3,2,1,0:T(8,128)S(1)} %get-tuple-element.19), channel_id=1, source_target_pairs={{16,0},{17,1},{18,2},{19,3},{20,4},{21,5},{22,6},{23,7},{24,8},{25... | collective-permute-start | bytes 786440 | tf_op jit(solution)/shard_map/ppermute | solution.py:20
  275.0 3.6 collective-permute-start.44
  277.3 3.5 collective-permute-start.45
  282.7 7.7 %collective-permute-start.46 = (f32[20,20,2,128]{3,2,1,0:T(2,128)}, f32[20,20,2,128]{3,2,1,0:T(2,128)}, u32[]{:S(2)}, u32[]{:S(2)}) collective-permute-start(f32[20,20,2,128]{3,2,1,0:T(2,128)} %get-tuple-element.11), channel_id=1, source_target_pairs={{0,1},{1,2},{2,3},{4,5},{5,6},{6,7},{8,9},{9,10},{10,11},{12,13},{... | collective-permute-start | bytes 1228808 | tf_op jit(solution)/shard_map/ppermute | solution.py:19
  285.4 10.4 %collective-permute-start.47 = (f32[20,20,2,128]{3,2,1,0:T(2,128)}, f32[20,20,2,128]{3,2,1,0:T(2,128)}, u32[]{:S(2)}, u32[]{:S(2)}) collective-permute-start(f32[20,20,2,128]{3,2,1,0:T(2,128)} %get-tuple-element.10), channel_id=1, source_target_pairs={{1,0},{2,1},{3,2},{5,4},{6,5},{7,6},{9,8},{10,9},{11,10},{13,12},{... | collective-permute-start | bytes 1228808 | tf_op jit(solution)/shard_map/ppermute | solution.py:20
  289.7 10.6 %copy-start.5 = (f32[16,16,16,64]{3,2,1,0:T(8,128)S(1)}, f32[16,16,16,64]{3,2,1,0:T(8,128)}, u32[]{:S(2)}) copy-start(f32[16,16,16,64]{3,2,1,0:T(8,128)} %copy-done.4) | copy-start | bytes 3145732
  289.7 10.6 %copy-start.11 = (f32[18,18,18]{2,1,0:T(8,128)S(1)}, f32[18,18,18]{2,1,0:T(8,128)}, u32[]{:S(2)}) copy-start(f32[18,18,18]{2,1,0:T(8,128)} %copy-done.10) | copy-start | bytes 69988
  313.0 2.9 copy-start.6
  (3 other events, 3.5 us)
